TPU v7x, 8 devices: a whole 2x2x1 slice. The times are simulated.
8 devices in a mesh: dp: 1 (over z), ep: 8 (over x, y, core).
Axes of the slice: x: 2, y: 2, z: 1, core: 2. Of those that a mesh axis runs over, the one named last changes fastest.
Arguments:
- x: bfloat16 [1, 8, 256, 7168], P('dp', 'ep')
- expert: int32 [1, 8, 256, 8], P('dp', 'ep')
- slot: int32 [1, 8, 256, 8], P('dp', 'ep')
- gate: float32 [1, 8, 256, 8], P('dp', 'ep')
- w_gate: bfloat16 [32, 7168, 2048], P('ep')
- w_up: bfloat16 [32, 7168, 2048], P('ep')
- w_down: bfloat16 [32, 2048, 7168], P('ep')
- s_gate: bfloat16 [7168, 2048], replicated
- s_up: bfloat16 [7168, 2048], replicated
- s_down: bfloat16 [2048, 7168], replicated
Outputs:
- y: bfloat16 [1, 8, 256, 7168], P('dp', 'ep')
All inputs are finite; a program needn't handle non-finite values.
Results may differ from a plain program's by a relative error of at most 0.009.
Values are sent between devices in bfloat16 or wider.
A program may use at most 2 GiB of HBM per device.

v0:
```python
import jax
import jax.numpy as jnp
from jax import lax
from jax.sharding import NamedSharding, PartitionSpec as P


def einsum(form, a, b):
    return jnp.einsum(form, a.astype(jnp.float32), b.astype(jnp.float32))


def for_all(x, s_gate, s_up, s_down):
    h = jax.nn.silu(einsum("...d,df->...f", x, s_gate)) * einsum("...d,df->...f", x, s_up)
    return einsum("...f,fd->...d", h.astype(jnp.bfloat16), s_down)


def solution(mesh):
    def placed(v, *spec):
        return lax.with_sharding_constraint(v, NamedSharding(mesh, P(*spec)))

    def step(x, expert, slot, gate, w_gate, w_up, w_down, s_gate, s_up, s_down):
        experts, (tokens, top) = w_gate.shape[0], expert.shape[2:]
        slots = 5 * tokens * top // (4 * experts)
        to_expert = jax.nn.one_hot(expert, experts, dtype=jnp.bfloat16)
        to_slot = jax.nn.one_hot(slot, slots, dtype=jnp.bfloat16)
        weighted = to_expert * gate[..., None].astype(jnp.bfloat16)
        dispatch = einsum("abtke,abtkc->abtec", to_expert, to_slot).astype(jnp.bfloat16)
        combine = einsum("abtke,abtkc->abtec", weighted, to_slot).astype(jnp.bfloat16)
        z = einsum("abtec,abtd->aebcd", dispatch, x).astype(jnp.bfloat16)
        z = placed(z, "dp", None, "ep", None, None)
        z = placed(z, "dp", "ep", None, None, None)
        h = jax.nn.silu(einsum("aebcd,edf->aebcf", z, w_gate))
        h = (h * einsum("aebcd,edf->aebcf", z, w_up)).astype(jnp.bfloat16)
        out = einsum("aebcf,efd->aebcd", h, w_down).astype(jnp.bfloat16)
        out = placed(out, "dp", "ep", None, None, None)
        out = placed(out, "dp", None, "ep", None, None)
        y = einsum("abtec,aebcd->abtd", combine, out)
        return (y + for_all(x, s_gate, s_up, s_down)).astype(jnp.bfloat16)

    return step
```

profile of v0, /device:TPU:0, one launch (start us, length us, event | category | flops | bytes accessed | tf_op | source)
XLA Modules:
  0.0 1166.9 jit_solution(13413307690436478104)
XLA Ops:
  0.0 0.8 copy.11
  0.8 0.0 copy-start.1
  0.8 0.8 copy.9
  1.7 0.0 copy-start.3
  1.7 2.6 convolution_convert_fusion.2
  4.3 18.4 %convolution_convert_fusion = bf16[32,80,7168]{2,1,0:T(8,128)(2,1)} fusion(bf16[1,1,256,7168]{3,2,1,0:T(8,128)(2,1)} %param.3, bf16[256,32,80]{2,1,0:T(8,128)(2,1)S(1)} %convolution_convert_fusion.2), kind=kOutput, calls=%fused_computation.11 | convolution fusion | flops 9413591040 | bytes 41680896 | tf_op jit(solution)/abtec,abtd->aebcd/dot_general | solution.py:8
  22.8 0.0 copy-done.1
  22.8 0.0 copy-done.3
  22.8 408.2 %all-to-all.4 = bf16[1,8,4,1,80,7168]{5,4,2,3,0,1:T(8,128)(2,1)} all-to-all(bf16[1,8,4,1,80,7168]{5,4,2,3,0,1:T(8,128)(2,1)} %bitcast.144), channel_id=1, replica_groups=mesh['dp'=1,'ep'=8] {'ep'}, dimensions={1} | all-to-all | bytes 73400320 | tf_op jit(solution)/sharding_constraint;jit(solution)/sharding_constraint | solution.py:18
  431.0 86.0 %fusion.2 = f32[4,8,80,2048]{3,2,1,0:T(8,128)} fusion(bf16[4,7168,2048]{2,1,0:T(8,128)(2,1)} %param.5, bf16[1,8,4,1,80,7168]{5,4,2,3,0,1:T(8,128)(2,1)} %all-to-all.4), kind=kOutput, calls=%fused_computation.2 | convolution fusion | flops 75161927680 | bytes 175112192 | tf_op jit(solution)/aebcd,edf->aebcf/dot_general | solution.py:8
  517.0 86.0 %fusion.4 = f32[4,8,80,2048]{3,2,1,0:T(8,128)} fusion(bf16[4,7168,2048]{2,1,0:T(8,128)(2,1)} %param.4, bf16[1,8,4,1,80,7168]{5,4,2,3,0,1:T(8,128)(2,1)} %all-to-all.4), kind=kOutput, calls=%fused_computation.4 | convolution fusion | flops 75161927680 | bytes 175112192 | tf_op jit(solution)/aebcd,edf->aebcf/dot_general | solution.py:8
  603.0 95.5 %convert_bitcast_fusion = bf16[1,4,8,1,80,7168]{5,4,2,1,3,0:T(8,128)(2,1)} fusion(bf16[4,2048,7168]{2,1,0:T(8,128)(2,1)} %param.6, f32[4,8,80,2048]{3,2,1,0:T(8,128)} %fusion.2, f32[4,8,80,2048]{3,2,1,0:T(8,128)} %fusion.4), kind=kOutput, calls=%fused_computation.8 | convolution fusion | flops 75211735040 | bytes 196083712 | tf_op jit(solution)/aebcf,efd->aebcd/dot_general | solution.py:8
  698.5 25.0 %copy.15 = bf16[1,4,8,1,80,7168]{5,4,1,3,0,2:T(8,128)(2,1)} copy(bf16[1,4,8,1,80,7168]{5,4,2,1,3,0:T(8,128)(2,1)} %convert_bitcast_fusion) | data formatting | bytes 73400320 | tf_op jit(solution)/sharding_constraint;jit(solution)/sharding_constraint | solution.py:18
  723.5 0.0 copy-start.4
  723.5 6.2 all-to-all-start.1
  729.8 0.1 copy.10
  729.9 3.0 convolution_convert_fusion.1
  733.0 0.0 copy-start
  733.0 14.5 %fusion.31 = f32[1,256,2048]{2,1,0:T(8,128)S(1)} fusion(bf16[7168,2048]{1,0:T(8,128)(2,1)} %param.7, bf16[1,1,256,7168]{3,2,1,0:T(8,128)(2,1)} %param.3), kind=kOutput, calls=%fused_computation.31 | convolution fusion | flops 7516192768 | bytes 35127296 | tf_op jit(solution)/...d,df->...f/dot_general | solution.py:8
  747.5 0.0 copy-done
  747.5 13.9 %fusion.37 = bf16[256,2048]{1,0:T(8,128)(2,1)S(1)} fusion(bf16[7168,2048]{1,0:T(8,128)(2,1)} %param.8, bf16[1,1,256,7168]{3,2,1,0:T(8,128)(2,1)S(1)} %copy-done, f32[1,256,2048]{2,1,0:T(8,128)S(1)} %fusion.31), kind=kOutput, calls=%fused_computation.33 | convolution fusion | flops 7519338496 | bytes 36175872 | tf_op jit(solution)/...d,df->...f/dot_general | solution.py:8
  761.4 364.8 %all-to-all-done.1 = bf16[1,4,8,1,80,7168]{5,4,1,3,0,2:T(8,128)(2,1)} async-done(((bf16[1,4,8,1,80,7168]{5,4,1,3,0,2:T(8,128)(2,1)}), bf16[1,4,8,1,80,7168]{5,4,1,3,0,2:T(8,128)(2,1)}, u32[]{:S(2)}, u32[]{:S(2)}) %all-to-all-start.1) | async-done | bytes 36700192 | tf_op jit(solution)/sharding_constraint;jit(solution)/sharding_constraint | solution.py:18
  1126.2 21.0 %convolution_bitcast_fusion = f32[256,7168]{1,0:T(8,128)} fusion(bf16[32,80,7168]{2,1,0:T(8,128)(2,1)} %bitcast.38, bf16[256,32,80]{2,1,0:T(8,128)(2,1)S(1)} %convolution_convert_fusion.1), kind=kOutput, calls=%fused_computation.20 | convolution fusion | flops 9395240960 | bytes 45350912 | tf_op jit(solution)/abtec,aebcd->abtd/dot_general | solution.py:8
  1147.2 19.7 %fusion.19 = bf16[1,1,256,7168]{3,2,1,0:T(8,128)(2,1)} fusion(f32[256,7168]{1,0:T(8,128)} %convolution_bitcast_fusion, bf16[256,2048]{1,0:T(8,128)(2,1)S(1)} %fusion.37, bf16[2048,7168]{1,0:T(8,128)(2,1)} %param.9), kind=kOutput, calls=%fused_computation.23 | convolution fusion | flops 7519862784 | bytes 41418752 | tf_op jit(solution)/...f,fd->...d/dot_general | solution.py:8
  (6 shorter events, 0.0 us)
Async XLA Ops:
  0.8 22.0 %copy-start.1 = (s32[256,8]{1,0:T(8,128)}, s32[256,8]{1,0:T(8,128)S(1)}, u32[]{:S(2)}) copy-start(s32[256,8]{1,0:T(8,128)S(1)} %copy.11) | copy-start | bytes 24580
  1.7 21.1 %copy-start.3 = (s32[256,8]{1,0:T(8,128)}, s32[256,8]{1,0:T(8,128)S(1)}, u32[]{:S(2)}) copy-start(s32[256,8]{1,0:T(8,128)S(1)} %copy.9) | copy-start | bytes 24580
  723.5 6.3 copy-start.5
  723.5 6.4 copy-start.2
  723.5 6.4 copy-start.4
  723.5 402.7 %all-to-all-start.1 = ((bf16[1,4,8,1,80,7168]{5,4,1,3,0,2:T(8,128)(2,1)}), bf16[1,4,8,1,80,7168]{5,4,1,3,0,2:T(8,128)(2,1)}, u32[]{:S(2)}, u32[]{:S(2)}) async-start(bf16[1,4,8,1,80,7168]{5,4,1,3,0,2:T(8,128)(2,1)} %copy.15), calls=%async_computation.1 | async-start | bytes 73400320 | tf_op jit(solution)/sharding_constraint;jit(solution)/sharding_constraint | solution.py:18
  733.0 14.5 %copy-start = (bf16[1,1,256,7168]{3,2,1,0:T(8,128)(2,1)S(1)}, bf16[1,1,256,7168]{3,2,1,0:T(8,128)(2,1)}, u32[]{:S(2)}) copy-start(bf16[1,1,256,7168]{3,2,1,0:T(8,128)(2,1)} %param.3) | copy-start | bytes 11010052
where the time goes:
time: 1170 us
  blocking collectives  408 us (35%)
  waiting for transfers between devices  365 us (31%)
  matrix products  361 us (31%)
  local copies, waits for them, and re-layouts  26.9 us (2%)
    another operation x1, blocking collectives, placed(): return lax.with_sharding_constraint(v, NamedSharding(mesh, P(*spec)))  408 us
    another operation x1, waiting for transfers between devices, placed(): return lax.with_sharding_constraint(v, NamedSharding(mesh, P(*spec)))  365 us
    dot_general x10, matrix products, einsum(): return jnp.einsum(form, a.astype(jnp.float32), b.astype(jnp.float32))  361 us
    another operation x1, local copies, waits for them, and re-layouts, placed(): return lax.with_sharding_constraint(v, NamedSharding(mesh, P(*spec)))  25 us
  transfers between devices with their start and end apart: 1, of which 1 were waited for; matrix products, arithmetic and copies ran while one was open for 3% of the time, Pallas kernels for 0%

commit v1 on v0

v1 whole, which is shorter than its diff:
```python
import jax
import jax.numpy as jnp
from jax import lax
from jax.experimental import pallas as pl
from jax.experimental.pallas import tpu as pltpu
from jax.sharding import PartitionSpec as P

MESH = pl.DeviceIdType.MESH
F32, BF16 = jnp.float32, jnp.bfloat16
N = 8
T = 256
D = 7168
FF = 2048
TOP = 8
E = 4
CAP = 80
SEG = E * CAP
ROWS = N * SEG
PER = N * CAP
KB = 512
NK = D // KB
NB = 512
CB = 512
HB = CB // 2
NC = D // CB
WRING = 3
DRING = 4


def around(me):
    i, j, c = me // 4, (me // 2) % 2, me % 2
    at = lambda i, j, c: i * 4 + j * 2 + c
    return at(i, j, 1 - c), at(1 - i, j, c), at(i, 1 - j, c), at(1 - i, 1 - j, c)


def greet(devices):
    barrier = pltpu.get_barrier_semaphore()
    for d in devices:
        pl.semaphore_signal(barrier, inc=1, device_id={"ep": d}, device_id_type=MESH)
    pl.semaphore_wait(barrier, len(devices))


def remote(src, dst, send, recv, to):
    return pltpu.make_async_remote_copy(
        src_ref=src, dst_ref=dst, send_sem=send, recv_sem=recv, device_id={"ep": to}, device_id_type=MESH
    )


def dot(a, b):
    return jnp.dot(a, b, preferred_element_type=F32)


def up_kernel(
    x, table, wg, wu, sg, su, xg, tables, h, sh,
    acc_g, acc_u, z, xv, wv, pick, tv,
    w_sem, xv_sem, out_sem, t_send, t_recv, o_send, o_recv, f_send, f_recv, c_send, c_recv,
):
    me = lax.axis_index("ep")
    cn, xn, yn, dg = around(me)
    others = [lax.rem(me + d, N) for d in range(1, N)]

    def weights(s, run):
        slot = lax.rem(s, WRING)

        def two(a, b):
            for half, ref in ((0, a), (1, b)):
                run(pltpu.make_async_copy(ref, wv.at[slot, half], w_sem.at[slot, half]))

        @pl.when(s < NK)
        def _():
            rows = pl.ds(pl.multiple_of(s * KB, KB), KB)
            two(sg.at[rows], su.at[rows])

        @pl.when(jnp.logical_and(s >= NK, s < NK + NK * E))
        def _():
            k, e = (s - NK) // E, (s - NK) % E
            rows = pl.ds(pl.multiple_of(k * KB, KB), KB)
            two(wg.at[e, rows], wu.at[e, rows])

    for s in range(WRING - 1):
        weights(s, lambda c: c.start())

    def cols(k):
        return pl.ds(pl.multiple_of(k * KB, KB), KB)

    for k in range(NK):
        pltpu.make_async_copy(x.at[:, cols(k)], xv.at[k // N, k % N], xv_sem.at[k // N, k % N]).start()

    greet(others)
    for i, d in enumerate(others):
        remote(table, tv.at[me], t_send.at[i], t_recv.at[N - 2 - i], d).start()
    keep = pltpu.make_async_copy(table, tv.at[me], out_sem.at[0])
    keep.start()

    def own(k, run):
        for i, d in enumerate((xn, yn, cn)):
            run(remote(x.at[:, cols(k)], xg.at[me, :, cols(k)], o_send.at[i, k], o_recv.at[i, k], d))

    def forward(k, run):
        p = lax.rem(k, 2)
        src, to = xn * (1 - p) + yn * p, yn * (1 - p) + xn * p
        part = xg.at[src, :, cols(k)]
        run(remote(part, part, f_send.at[k], f_recv.at[k], to))

    def across(i, src, k, run):
        part = xg.at[src, :, cols(k)]
        run(remote(part, part, c_send.at[i, k], c_recv.at[i, k], cn))

    start, wait_send, wait_recv = (lambda c: c.start()), (lambda c: c.wait_send()), (lambda c: c.wait_recv())

    def arrived(i, src, k):
        part = xg.at[src, :, cols(k)]
        remote(part, part, o_send.at[i, k], o_recv.at[i, k], xn).wait_recv()

    def stage_own(k):
        @pl.when(k < NK)
        def _():
            own(k, start)

    def stage_forward(k):
        @pl.when(k < NK)
        def _():
            arrived(0, xn, k)
            arrived(1, yn, k)
            forward(k, start)
            across(0, xn, k, start)
            across(1, yn, k, start)

    def stage_across(k):
        @pl.when(k < NK)
        def _():
            part = xg.at[dg, :, cols(k)]
            remote(part, part, f_send.at[k], f_recv.at[k], xn).wait_recv()
            across(2, dg, k, start)

    def tokens(k, run):
        slot = lax.rem(k, 2)
        for d in range(1, N):
            b = lax.rem(me + d, N)
            run(pltpu.make_async_copy(xg.at[b, :, cols(k)], xv.at[slot, b], xv_sem.at[slot, b]))
        run(pltpu.make_async_copy(x.at[:, cols(k)], xv.at[slot, me], xv_sem.at[slot, me]))

    def stage_tokens(k):
        @pl.when(k < NK)
        def _():
            arrived(2, cn, k)
            for i in range(3):
                part = xg.at[cn, :, cols(k)]
                remote(part, part, c_send.at[i, k], c_recv.at[i, k], cn).wait_recv()
            tokens(k, start)

    stage_own(0)
    stage_own(1)

    def block(n):
        return pl.ds(pl.multiple_of(n * NB, NB), NB)

    def shared(s, first):
        weights(s + WRING - 1, lambda c: c.start())
        weights(s, lambda c: c.wait())
        a = (s // N, lax.rem(s, N))
        pltpu.make_async_copy(x.at[:, cols(s)], xv.at[a], xv_sem.at[a]).wait()
        slot = lax.rem(s, WRING)

        for n in range(FF // NB):
            for half, acc in ((0, acc_g), (1, acc_u)):
                b = slice(n * NB, (n + 1) * NB)
                v = dot(xv[a], wv[slot, half, :, b])
                acc[:T, b] = v if first else acc[:T, b] + v

    shared(0, True)

    def shared_body(s, c):
        @pl.when(s == NK // 2)
        def _():
            stage_forward(0)
            stage_own(2)

        shared(s, False)
        return c

    lax.fori_loop(1, NK, shared_body, 0)

    def shared_out(n, run):
        run(pltpu.make_async_copy(z.at[n * T:(n + 1) * T], sh.at[:, n * NB:(n + 1) * NB], out_sem.at[n]))

    keep.wait()
    for n in range(FF // NB):
        b = slice(n * NB, (n + 1) * NB)
        z[n * T:(n + 1) * T] = (jax.nn.silu(acc_g[:T, b]) * acc_u[:T, b]).astype(BF16)

    for i in range(N - 1):
        b = lax.rem(me + 1 + i, N)
        remote(table, tv.at[b], t_send.at[i], t_recv.at[i], b).wait_recv()
    for n in range(FF // NB):
        shared_out(n, lambda c: c.start())
    row = (lax.broadcasted_iota(jnp.int32, (SEG, T), 0) + me * SEG).astype(F32)

    def picks(b, c):
        hit = jnp.zeros((SEG, T), F32)
        for j in range(TOP):
            hit = hit + jnp.where(tv[b, j:j + 1, :] == row, 1.0, 0.0)
        pick[b] = hit.astype(BF16)
        return c

    lax.fori_loop(0, N, picks, 0)
    keep_tables = pltpu.make_async_copy(tv, tables, xv_sem.at[2, 0])
    keep_tables.start()
    for n in range(FF // NB):
        shared_out(n, lambda c: c.wait())

    stage_forward(1)
    stage_own(3)
    stage_across(0)
    stage_tokens(0)

    def gather(k):
        slot = lax.rem(k, 2)
        tokens(k, lambda c: c.wait())

        for b in range(N):
            v = dot(pick[b], xv[slot, b]).astype(BF16)
            for e in range(E):
                z[e * PER + b * CAP:e * PER + (b + 1) * CAP] = v[e * CAP:(e + 1) * CAP]

    def expert(k, e, first):
        s = NK + k * E + e
        weights(s + WRING - 1, lambda c: c.start())
        weights(s, lambda c: c.wait())
        slot = lax.rem(s, WRING)
        rows = pl.ds(pl.multiple_of(e * PER, PER), PER)

        for n in range(FF // NB):
            for half, acc in ((0, acc_g), (1, acc_u)):
                b = slice(n * NB, (n + 1) * NB)
                v = dot(z[rows], wv[slot, half, :, b])
                acc[rows, b] = v if first else acc[rows, b] + v

    def chunk(k, first):
        gather(k)

        def body(e, c):
            expert(k, e, first)

            @pl.when(e == 0)
            def _():
                stage_forward(k + 2)
                stage_own(k + 4)

            @pl.when(e == 1)
            def _():
                stage_across(k + 1)

            @pl.when(e == 2)
            def _():
                stage_tokens(k + 1)

            return c

        lax.fori_loop(0, E, body, 0)

    chunk(0, True)

    def chunks(k, c):
        chunk(k, False)
        return c

    lax.fori_loop(1, NK, chunks, 0)

    def store(n, e, run):
        rows = pl.ds(pl.multiple_of(e * PER, PER), PER)
        run(pltpu.make_async_copy(z.at[rows], h.at[rows, block(n)], out_sem.at[e]))

    def finish(i, c):
        n, e = i // E, lax.rem(i, E)
        rows = pl.ds(pl.multiple_of(e * PER, PER), PER)

        @pl.when(n > 0)
        def _():
            store(n - 1, e, lambda c: c.wait())

        z[rows] = (jax.nn.silu(acc_g[rows, block(n)]) * acc_u[rows, block(n)]).astype(BF16)
        store(n, e, lambda c: c.start())
        return c

    lax.fori_loop(0, FF // NB * E, finish, 0)
    for e in range(E):
        store(FF // NB - 1, e, lambda c: c.wait())
    keep_tables.wait()
    for i, d in enumerate(others):
        remote(table, tv.at[me], t_send.at[i], t_recv.at[i], d).wait_send()

    def drain(k, c):
        own(k, wait_send)
        forward(k, wait_send)
        for i, src in enumerate((xn, yn, dg)):
            across(i, src, k, wait_send)
        return c

    lax.fori_loop(0, NK, drain, 0)


def down_kernel(
    h, tables, wd, sh, sd, y,
    hv, wv, sv, shv, tv, comb, out, d_out, d_in, p_out, p_in, q_out, q_in, yv,
    h_sem, w_sem, s_sem, m_sem, y_sem, d_send, d_recv, p_send, p_recv, q_send, q_recv,
):
    me = lax.axis_index("ep")
    cn, xn, yn, dg = around(me)

    def cols(n):
        return pl.ds(pl.multiple_of(n * CB, CB), CB)

    def weights(s, run):
        @pl.when(s < NC * E)
        def _():
            slot = lax.rem(s, DRING)
            run(pltpu.make_async_copy(wd.at[s % E, :, cols(s // E)], wv.at[slot], w_sem.at[slot]))

    def shared(n, run):
        slot = lax.rem(n, 2)
        run(pltpu.make_async_copy(sd.at[:, cols(n)], sv.at[slot], s_sem.at[slot]))

    def activations(e, run):
        rows = pl.ds(pl.multiple_of(e * PER, PER), PER)
        run(pltpu.make_async_copy(h.at[rows], hv.at[rows], h_sem.at[e]))

    start, wait = (lambda c: c.start()), (lambda c: c.wait())
    load_tables = pltpu.make_async_copy(tables, tv, m_sem.at[0])
    load_tables.start()
    load_sh = pltpu.make_async_copy(sh, shv, m_sem.at[1])
    for e in range(E):
        activations(e, start)
        if e < DRING - 1:
            weights(e, start)
    load_sh.start()
    greet((cn, xn, yn))

    load_tables.wait()
    wide = -(-SEG // 128) * 128
    row = (lax.broadcasted_iota(jnp.int32, (wide, T), 0) + me * SEG).astype(F32)
    inside = lax.broadcasted_iota(jnp.int32, (wide, T), 0) < SEG

    def combines(b, c):
        v = jnp.zeros((wide, T), F32)
        for j in range(TOP):
            v = v + jnp.where(tv[b, j:j + 1, :] == row, tv[b, TOP + j:TOP + j + 1, :], 0.0)
        comb[b] = jnp.where(inside, v, 0.0).T.astype(BF16)
        return c

    lax.fori_loop(0, N, combines, 0)
    load_sh.wait()

    def product(i):
        slot = lax.rem(i, 4)

        def body(e, c):
            s = i * E + e
            weights(s + DRING - 1, start)
            weights(s, wait)

            @pl.when(i == 0)
            def _():
                activations(e, wait)

            rows = pl.ds(pl.multiple_of(e * PER, PER), PER)
            v = dot(hv[rows], wv[lax.rem(s, DRING)]).astype(BF16)
            for b in range(N):
                out[slot, b, pl.ds(pl.multiple_of(e * CAP, 16), CAP)] = v[b * CAP:(b + 1) * CAP]
            return c

        lax.fori_loop(0, E, body, 0)

    def summed(b, n, lanes):
        return dot(comb[b][:, :SEG], out[lax.rem(n, 4), b, :, lanes])

    both, left, right = slice(0, CB), slice(0, HB), slice(HB, CB)

    def to_partner(n, run):
        slot = lax.rem(n, 2)
        run(remote(d_out.at[slot], d_in.at[lax.rem(n, 5)], d_send.at[slot], d_recv.at[n], cn))

    def first_hop(n, run):
        slot = lax.rem(n, 2)
        for i, d in enumerate((xn, yn)):
            run(remote(p_out.at[slot, i], p_in.at[n, i], p_send.at[slot, i], p_recv.at[n, i], d))

    def second_hop(n, run):
        slot = lax.rem(n, 2)
        for i, d in enumerate((yn, xn)):
            run(remote(q_out.at[slot, i], q_in.at[n, i], q_send.at[slot, i], q_recv.at[n, i], d))

    wait_send, wait_recv = (lambda c: c.wait_send()), (lambda c: c.wait_recv())

    def for_partner(n):
        cx, cy, cd = around(cn)[1:]
        slot = lax.rem(n, 2)

        @pl.when(n >= 2)
        def _():
            to_partner(n - 2, wait_send)

        for i, b in enumerate((cn, cx, cy, cd)):
            d_out[slot, i] = summed(b, n, both).astype(BF16)

    def for_first(n):
        slot, held = lax.rem(n, 2), lax.rem(n, 5)

        @pl.when(n >= 2)
        def _():
            first_hop(n - 2, wait_send)

        to_partner(n, wait_recv)
        v = (summed(dg, n, both) + d_in[held, 3].astype(F32)).astype(BF16)
        p_out[slot, 0, 1] = v[:, :HB]
        p_out[slot, 1, 1] = v[:, HB:]
        for i, (b, at, lanes) in enumerate(((xn, 1, left), (yn, 2, right))):
            p_out[slot, i, 0] = (summed(b, n, lanes) + d_in[held, at, :, lanes].astype(F32)).astype(BF16)

    def for_second(n):
        slot, held = lax.rem(n, 2), lax.rem(n, 5)

        @pl.when(n >= 2)
        def _():
            second_hop(n - 2, wait_send)

        first_hop(n, wait_recv)
        for i, (b, at, lanes) in enumerate(((yn, 2, left), (xn, 1, right))):
            v = summed(b, n, lanes) + d_in[held, at, :, lanes].astype(F32) + p_in[n, i, 1].astype(F32)
            q_out[slot, i] = v.astype(BF16)

    def result(n, run):
        slot = lax.rem(n, 2)
        run(pltpu.make_async_copy(yv.at[slot], y.at[:, cols(n)], y_sem.at[slot]))

    def for_own(n):
        slot, held = lax.rem(n, 2), lax.rem(n, 5)

        @pl.when(n >= 2)
        def _():
            result(n - 2, wait)

        shared(n, wait)
        v = dot(shv[...], sv[lax.rem(n, 2)])
        v = v + summed(me, n, both) + d_in[held, 0].astype(F32)
        second_hop(n, wait_recv)
        for i, lanes in enumerate((left, right)):
            w = v[:, lanes] + p_in[n, i, 0].astype(F32) + q_in[n, i].astype(F32)
            yv[slot, :, lanes] = w.astype(BF16)
        result(n, start)

    def when_chunk(n, f):
        @pl.when(jnp.logical_and(n >= 0, n < NC))
        def _():
            f(n)

    def step(i, c):
        @pl.when(jnp.logical_and(i >= 2, i - 2 < NC))
        def _():
            shared(i - 2, start)

        when_chunk(i, product)
        when_chunk(i, for_partner)
        when_chunk(i - 1, for_first)
        when_chunk(i, lambda n: to_partner(n, start))
        when_chunk(i - 2, for_second)
        when_chunk(i - 1, lambda n: first_hop(n, start))
        when_chunk(i - 3, for_own)
        when_chunk(i - 2, lambda n: second_hop(n, start))
        return c

    lax.fori_loop(0, NC + 3, step, 0)
    for n in (NC - 2, NC - 1):
        to_partner(n, wait_send)
        first_hop(n, wait_send)
        second_hop(n, wait_send)
        result(n, wait)


ANY = pl.BlockSpec(memory_space=pl.ANY)
VMEM_LIMIT = 67043328


def up(x, table, wg, wu, sg, su):
    dma = pltpu.SemaphoreType.DMA
    return pl.pallas_call(
        up_kernel,
        name="up",
        out_shape=(
            jax.ShapeDtypeStruct((N, T, D), BF16),
            jax.ShapeDtypeStruct((N, 2 * TOP, T), F32),
            jax.ShapeDtypeStruct((ROWS, FF), BF16),
            jax.ShapeDtypeStruct((T, FF), BF16),
        ),
        in_specs=[ANY] * 6,
        out_specs=(ANY,) * 4,
        scratch_shapes=[
            pltpu.VMEM((ROWS, FF), F32),
            pltpu.VMEM((ROWS, FF), F32),
            pltpu.VMEM((ROWS, KB), BF16),
            pltpu.VMEM((2, N, T, KB), BF16),
            pltpu.VMEM((WRING, 2, KB, FF), BF16),
            pltpu.VMEM((N, SEG, T), BF16),
            pltpu.VMEM((N, 2 * TOP, T), F32),
            dma((WRING, 2)),
            dma((3, N)),
            dma((4,)),
            dma((N - 1,)),
            dma((N - 1,)),
            dma((3, NK)),
            dma((3, NK)),
            dma((NK,)),
            dma((NK,)),
            dma((3, NK)),
            dma((3, NK)),
        ],
        compiler_params=pltpu.CompilerParams(collective_id=0, has_side_effects=True, vmem_limit_bytes=VMEM_LIMIT),
    )(x, table, wg, wu, sg, su)


def down(h, tables, wd, sh, sd):
    dma = pltpu.SemaphoreType.DMA
    return pl.pallas_call(
        down_kernel,
        name="down",
        out_shape=jax.ShapeDtypeStruct((T, D), BF16),
        in_specs=[ANY] * 5,
        out_specs=ANY,
        scratch_shapes=[
            pltpu.VMEM((ROWS, FF), BF16),
            pltpu.VMEM((DRING, FF, CB), BF16),
            pltpu.VMEM((2, FF, CB), BF16),
            pltpu.VMEM((T, FF), BF16),
            pltpu.VMEM((N, 2 * TOP, T), F32),
            pltpu.VMEM((N, T, -(-SEG // 128) * 128), BF16),
            pltpu.VMEM((4, N, SEG, CB), BF16),
            pltpu.VMEM((2, 4, T, CB), BF16),
            pltpu.VMEM((5, 4, T, CB), BF16),
            pltpu.VMEM((2, 2, 2, T, HB), BF16),
            pltpu.VMEM((NC, 2, 2, T, HB), BF16),
            pltpu.VMEM((2, 2, T, HB), BF16),
            pltpu.VMEM((NC, 2, T, HB), BF16),
            pltpu.VMEM((2, T, CB), BF16),
            dma((E,)),
            dma((DRING,)),
            dma((2,)),
            dma((2,)),
            dma((2,)),
            dma((2,)),
            dma((NC,)),
            dma((2, 2)),
            dma((NC, 2)),
            dma((2, 2)),
            dma((NC, 2)),
        ],
        compiler_params=pltpu.CompilerParams(collective_id=1, has_side_effects=True, vmem_limit_bytes=VMEM_LIMIT),
    )(h, tables, wd, sh, sd)


def solution(mesh):
    def device(x, expert, slot, gate, wg, wu, wd, sg, su, sd):
        key = jnp.where(slot < CAP, expert * CAP + slot, -1)[0, 0]
        weight = gate.astype(BF16)[0, 0]
        table = jnp.concatenate([key.T.astype(F32), weight.T.astype(F32)])
        _, tables, h, sh = up(x[0, 0], table, wg, wu, sg, su)
        return down(h, tables, wd, sh, sd)[None, None]

    tokens, experts = P("dp", "ep"), P("ep")
    return jax.shard_map(
        device,
        mesh=mesh,
        in_specs=(tokens,) * 4 + (experts,) * 3 + (P(),) * 3,
        out_specs=tokens,
        check_vma=False,
    )
```

time: 1170 us -> 372 us (0.32)
  blocking collectives: 408 us -> 0 us
  Pallas kernels: 0 us -> 365 us
  waiting for transfers between devices: 365 us -> 0 us
  matrix products: 361 us -> 0 us
  local copies, waits for them, and re-layouts: 26.9 us -> 4.11 us
    another operation x1 -> x0, blocking collectives: 408 us -> none  [placed(): return lax.with_sharding_constraint(v, NamedSharding(mesh, P(*spec)))]
    pallas_call x0 -> x2, Pallas kernels: none -> 365 us  [the longest x1 216 us: up(): pl.pallas_call(up_kernel, name='up', out_shape=(jax.ShapeDtypeStruct((N,...]
    another operation x1 -> x0, waiting for transfers between devices: 365 us -> none  [placed(): return lax.with_sharding_constraint(v, NamedSharding(mesh, P(*spec)))]
    dot_general x10 -> x0, matrix products: 361 us -> none  [einsum(): return jnp.einsum(form, a.astype(jnp.float32), b.astype(jnp.float32))]
    another operation x1 -> x0, local copies, waits for them, and re-layouts: 25 us -> none  [placed(): return lax.with_sharding_constraint(v, NamedSharding(mesh, P(*spec)))]
  transfers between devices with their start and end apart: 1 -> 0, of which waited for: 1 -> 0; matrix products, arithmetic and copies ran while one was open for 3% -> 0% of each run, Pallas kernels for 0% -> 0%
where the time goes in v1:
time: 372 us
  Pallas kernels  365 us (98%)
  local copies, waits for them, and re-layouts  4.11 us (1%)
    pallas_call x1, Pallas kernels, up(): pl.pallas_call(up_kernel, name='up', out_shape=(jax.ShapeDtypeStruct((N,...  216 us
    pallas_call x1, Pallas kernels, down(): pl.pallas_call(down_kernel, name='down', out_shape=jax.ShapeDtypeStruct((...  149 us

profile of v1, /device:TPU:0, one launch (start us, length us, event | category | flops | bytes accessed | tf_op | source)
XLA Modules:
  0.0 371.6 jit_solution(941270037268785463)
XLA Ops:
  0.0 0.7 convert_bitcast_fusion.1
  0.7 0.7 convert_bitcast_fusion
  1.4 0.6 pad_maximum_fusion.table
  2.0 216.1 %up.1 = (bf16[8,256,7168]{2,1,0:T(8,128)(2,1)}, f32[8,16,256]{2,1,0:T(8,128)}, bf16[2560,2048]{1,0:T(8,128)(2,1)}, bf16[256,2048]{1,0:T(8,128)(2,1)}) custom-call(bf16[256,7168]{1,0:T(8,128)(2,1)} %bitcast.12, f32[16,256]{1,0:T(8,128)} %pad_maximum_fusion.table, bf16[4,7168,2048]{2,1,0:T(8,128)(2,1)} %wg.1, bf16[4,7168,2048]{2,1,0:T(8,128)(2,1)} %wu.1, ...), custom_call_target="tpu_custom_call" | custom-call | tf_op jit(solution)/shard_map/up/pallas_call | solution.py:486
  218.1 149.3 %down.1 = bf16[256,7168]{1,0:T(8,128)(2,1)} custom-call(bf16[2560,2048]{1,0:T(8,128)(2,1)} %get-tuple-element.8.h, f32[8,16,256]{2,1,0:T(8,128)} %get-tuple-element.9.tables, bf16[4,2048,7168]{2,1,0:T(8,128)(2,1)} %wd.1, bf16[256,2048]{1,0:T(8,128)(2,1)} %get-tuple-element.10.sh, bf16[2048,7168]{1,0:T(8,128)(2,1)} %sd.1), custom_call_target="tpu_custom_call" | custom-call | tf_op jit(solution)/shard_map/down/pallas_call | solution.py:523
  367.4 4.1 %copy.12 = bf16[1,1,256,7168]{3,2,1,0:T(8,128)(2,1)} copy(bf16[1,1,256,7168]{3,2,1,0:T(8,128)(2,1)} %bitcast.11) | data formatting | bytes 7340032

commit v2 on v0

v2 whole, which is shorter than its diff:
```python
import functools

import jax
import jax.numpy as jnp
from jax import lax
from jax.experimental import pallas as pl
from jax.experimental.pallas import tpu as pltpu
from jax.sharding import PartitionSpec as P

MESH = pl.DeviceIdType.MESH
F32, BF16 = jnp.float32, jnp.bfloat16
N = 8
T = 256
D = 7168
FF = 2048
TOP = 8
E = 4
EXPERTS = N * E
CAP = 80
SEG = E * CAP
KB = 512
NK = D // KB
EARLY = 2
NB = 512
CB = 512
HB = CB // 2
NC = D // CB
SRING = 4
ROWS = 3 * TOP
FULL = (CAP,) * E
NARROW = (80, 80, 80, 32)
VMEM_LIMIT = 67043328

start, wait = (lambda c: c.start()), (lambda c: c.wait())
wait_send, wait_recv = (lambda c: c.wait_send()), (lambda c: c.wait_recv())


def around(me):
    i, j, c = me // 4, (me // 2) % 2, me % 2
    at = lambda i, j, c: i * 4 + j * 2 + c
    return at(i, j, 1 - c), at(1 - i, j, c), at(i, 1 - j, c), at(1 - i, 1 - j, c)


def greet(devices):
    barrier = pltpu.get_barrier_semaphore()
    for d in devices:
        pl.semaphore_signal(barrier, inc=1, device_id={"ep": d}, device_id_type=MESH)
    pl.semaphore_wait(barrier, len(devices))


def remote(src, dst, send, recv, to):
    return pltpu.make_async_remote_copy(
        src_ref=src, dst_ref=dst, send_sem=send, recv_sem=recv, device_id={"ep": to}, device_id_type=MESH
    )


def dot(a, b):
    return jnp.dot(a, b, preferred_element_type=F32)


def cols(k):
    return pl.ds(pl.multiple_of(k * KB, KB), KB)


class Way:
    def __init__(self, x, xg, sems):
        self.x, self.xg = x, xg
        self.o_send, self.o_recv, self.f_send, self.f_recv, self.c_send, self.c_recv = sems
        self.me = lax.axis_index("ep")
        self.cn, self.xn, self.yn, self.dg = around(self.me)

    def part(self, b, k):
        return self.xg.at[b, :, cols(k)]

    def own(self, k, run):
        for i, d in enumerate((self.xn, self.yn, self.cn)):
            run(remote(self.x.at[:, cols(k)], self.part(self.me, k), self.o_send.at[i, k], self.o_recv.at[i, k], d))

    def onward(self, k, run):
        p = lax.rem(k, 2)
        src, to = self.xn * (1 - p) + self.yn * p, self.yn * (1 - p) + self.xn * p
        run(remote(self.part(src, k), self.part(src, k), self.f_send.at[k], self.f_recv.at[k], to))

    def across(self, i, src, k, run):
        part = self.part(src, k)
        run(remote(part, part, self.c_send.at[i, k], self.c_recv.at[i, k], self.cn))

    def arrived(self, i, src, k):
        part = self.part(src, k)
        remote(part, part, self.o_send.at[i, k], self.o_recv.at[i, k], src).wait_recv()

    def forward(self, k):
        self.arrived(0, self.xn, k)
        self.arrived(1, self.yn, k)
        self.onward(k, start)
        self.across(0, self.xn, k, start)
        self.across(1, self.yn, k, start)

    def landed(self, k):
        part = self.part(self.dg, k)
        remote(part, part, self.f_send.at[k], self.f_recv.at[k], self.xn).wait_recv()

    def hand_over(self, k):
        self.landed(k)
        self.across(2, self.dg, k, start)

    def across_landed(self, i, k):
        part = self.part(self.cn, k)
        remote(part, part, self.c_send.at[i, k], self.c_recv.at[i, k], self.cn).wait_recv()

    def complete(self, k):
        self.arrived(2, self.cn, k)
        for i in range(3):
            self.across_landed(i, k)

    def passed_on(self, k, run):
        self.onward(k, run)
        for i, src in enumerate((self.xn, self.yn, self.dg)):
            self.across(i, src, k, run)


def way_semaphores(chunks):
    dma = pltpu.SemaphoreType.DMA
    return [dma((3, chunks)), dma((3, chunks)), dma((chunks,)), dma((chunks,)), dma((3, chunks)), dma((3, chunks))]


def share_kernel(
    expert, slot, gate, x, sg, su, xg, tables, plan, sh,
    mine, tv, pv, xv, wv, acc_g, acc_u, hv, x_sem, w_sem, h_sem, t_send, t_recv, *sems,
):
    me = lax.axis_index("ep")
    others = [lax.rem(me + d, N) for d in range(1, N)]
    way = Way(x, xg, sems)

    def weights(s, run):
        at = lax.rem(s, SRING)
        for half, ref in ((0, sg), (1, su)):
            run(pltpu.make_async_copy(ref.at[cols(s)], wv.at[at, half], w_sem.at[at, half]))

    def tokens(s, run):
        run(pltpu.make_async_copy(x.at[:, cols(s)], xv.at[s], x_sem.at[s]))

    for s in range(SRING - 1):
        tokens(s, start)
        weights(s, start)

    key = jnp.where(slot[...] < CAP, expert[...] * CAP + slot[...], -1).astype(F32)
    mine[:TOP] = key
    mine[TOP:2 * TOP] = gate[...].astype(BF16).astype(F32)
    key = jnp.concatenate([key, jnp.zeros((128 - TOP, T), F32)]).T
    low = (lax.broadcasted_iota(jnp.int32, (T, 128), 1) * CAP).astype(F32)
    used = jnp.zeros((T, 128), F32)
    for j in range(TOP):
        depth = key[:, j:j + 1] - low
        used = jnp.maximum(used, jnp.where((depth >= 0) & (depth < CAP), depth + 1, 0.0))
    used = jnp.max(used, axis=0, keepdims=True)
    mine[2 * TOP:] = jnp.broadcast_to(jnp.concatenate([used, used], axis=1), (TOP, T))

    greet(others)
    for k in range(EARLY):
        way.own(k, start)
    for i, d in enumerate(others):
        remote(mine, tv.at[me], t_send.at[i], t_recv.at[N - 2 - i], d).start()
    for s in range(SRING - 1, NK):
        tokens(s, start)
    tv[me] = mine[...]

    def step(s, first):
        @pl.when(s + SRING - 1 < NK)
        def _():
            weights(s + SRING - 1, start)

        tokens(s, wait)
        weights(s, wait)
        for n in range(FF // NB):
            b = slice(n * NB, (n + 1) * NB)
            for half, acc in ((0, acc_g), (1, acc_u)):
                v = dot(xv[s], wv[lax.rem(s, SRING), half, :, b])
                acc[:, b] = v if first else acc[:, b] + v

    step(0, True)

    def body(s, c):
        step(s, False)

        @pl.when(s == 5)
        def _():
            way.forward(0)

        @pl.when(s == 9)
        def _():
            way.forward(1)

        return c

    lax.fori_loop(1, NK, body, 0)
    for i in range(N - 1):
        b = lax.rem(me + 1 + i, N)
        remote(mine, tv.at[b], t_send.at[i], t_recv.at[i], b).wait_recv()
    keep = pltpu.make_async_copy(tv, tables, h_sem.at[0])
    keep.start()
    way.hand_over(0)

    n = tv[0, 2 * TOP:, :128]
    for b in range(1, N):
        n = jnp.maximum(n, tv[b, 2 * TOP:, :128])
    lane = lax.broadcasted_iota(jnp.int32, n.shape, 1)
    e = lane % E
    rank = jnp.zeros(n.shape, jnp.int32)
    for o in range(1, E):
        later = e + o < E
        other = jnp.where(later, pltpu.roll(n, 128 - o, 1), pltpu.roll(n, E - o, 1))
        rank = rank + ((other > n) | ((other == n) & jnp.logical_not(later))).astype(jnp.int32)
    caps = jnp.zeros(n.shape, F32)
    for r in range(E):
        caps = jnp.where(rank == r, float(NARROW[r]), caps)
    over = jnp.where((n > caps) & (lane < EXPERTS), 1.0, 0.0)
    out = jnp.where(lane == E, jnp.max(over, axis=1, keepdims=True), 0.0)
    for r in range(E):
        chosen = jnp.where((lane // E == me) & (rank == r), e, 0).astype(F32)
        out = out + jnp.where(lane == r, jnp.sum(chosen, axis=1, keepdims=True), 0.0)
    pv[...] = out.astype(jnp.int32)

    hv[...] = (jax.nn.silu(acc_g[...]) * acc_u[...]).astype(BF16)
    keep_plan = pltpu.make_async_copy(pv, plan, h_sem.at[2])
    keep_plan.start()
    keep_sh = pltpu.make_async_copy(hv, sh, h_sem.at[1])
    keep_sh.start()
    for i, d in enumerate(others):
        remote(mine, tv.at[me], t_send.at[i], t_recv.at[N - 2 - i], d).wait_send()
    way.complete(0)
    way.across(2, way.dg, 0, wait_send)
    way.arrived(2, way.cn, 1)
    way.landed(1)
    for k in range(EARLY):
        way.own(k, wait_send)
        way.onward(k, wait_send)
        for i, src in enumerate((way.xn, way.yn)):
            way.across(i, src, k, wait_send)
    for i in range(2):
        way.across_landed(i, 1)
    keep.wait()
    keep_plan.wait()
    keep_sh.wait()


def bases(caps):
    return [sum(caps[:r]) for r in range(E)]


def ranks(caps, plan):
    return list(range(E)) if caps == FULL else [plan[0, r] for r in range(E)]


def up_kernel(
    caps, plan, x, _, tables, wg, wu, xg, h, acc_g, acc_u, z, xv, w0, w1, pick, tv, w_sem, x_sem, z_sem, t_sem, *sems
):
    seg, at = sum(caps), bases(caps)
    wv = (w0, w1)
    width = w0.shape[-1]
    parts = FF // width
    me = lax.axis_index("ep")
    way = Way(x, xg, sems)
    perm = ranks(caps, plan)

    def weights(s, slot, run):
        @pl.when(s < NK * parts)
        def _():
            k, lanes = s // parts, pl.ds(pl.multiple_of(lax.rem(s, parts) * width, width), width)
            for e in range(E):
                for half, ref in ((0, wg), (1, wu)):
                    run(pltpu.make_async_copy(ref.at[e, cols(k), lanes], wv[slot].at[e, half], w_sem.at[slot, e, half]))

    def tokens(k, run):
        slot = lax.rem(k, 2)

        @pl.when(k < NK)
        def _():
            for d in range(1, N):
                b = lax.rem(me + d, N)
                run(pltpu.make_async_copy(way.part(b, k), xv.at[slot, b], x_sem.at[slot, b]))
            run(pltpu.make_async_copy(x.at[:, cols(k)], xv.at[slot, me], x_sem.at[slot, me]))

    load_tables = pltpu.make_async_copy(tables, tv, t_sem)
    load_tables.start()
    tokens(0, start)
    weights(0, 0, start)
    greet((way.cn, way.xn, way.yn))
    way.across(2, way.dg, EARLY - 1, start)
    for k in range(EARLY, EARLY + 2):
        way.own(k, start)

    load_tables.wait()
    first_key = [(me * E + perm[r]) * CAP for r in range(E)]

    def picks(b, c):
        for r in range(E):
            key = (lax.broadcasted_iota(jnp.int32, (caps[r], T), 0) + first_key[r]).astype(F32)
            hit = jnp.zeros((caps[r], T), F32)
            for j in range(TOP):
                hit = hit + jnp.where(tv[b, j:j + 1, :] == key, 1.0, 0.0)
            pick[b, at[r]:at[r] + caps[r]] = hit.astype(BF16)
        return c

    lax.fori_loop(0, N, picks, 0)

    def clear(i, c):
        rows = pl.ds(pl.multiple_of(i * 16, 16), 16)
        acc_g[rows] = jnp.zeros((16, FF), F32)
        acc_u[rows] = jnp.zeros((16, FF), F32)
        return c

    lax.fori_loop(0, N * seg // 16, clear, 0)

    def gather(k):
        slot = lax.rem(k, 2)
        tokens(k, wait)
        for b in range(N):
            v = dot(pick[b], xv[slot, b]).astype(BF16)
            for r in range(E):
                z[N * at[r] + b * caps[r]:N * at[r] + (b + 1) * caps[r]] = v[at[r]:at[r] + caps[r]]

    def product(k, j, slot):
        s = k * parts + j
        weights(s + 1, 1 - slot, start)
        weights(s, slot, wait)
        for n in range(width // NB):
            b = pl.ds(pl.multiple_of(j * width + n * NB, NB), NB)
            for r in range(E):
                rows = slice(N * at[r], N * (at[r] + caps[r]))
                for half, acc in ((0, acc_g), (1, acc_u)):
                    acc[rows, b] = acc[rows, b] + dot(
                        z[rows], wv[slot][perm[r], half, :, n * NB:(n + 1) * NB]
                    )

    def bring(k):
        @pl.when(k < NK)
        def _():
            @pl.when(k >= EARLY)
            def _():
                way.complete(k)

            @pl.when(k == EARLY - 1)
            def _():
                way.across_landed(2, k)

            tokens(k, start)

    def middle(k):
        @pl.when(k == 0)
        def _():
            way.forward(EARLY)

        @pl.when(k + 4 < NK)
        def _():
            way.own(k + 4, start)

        bring(k + 1)

    def end(k):
        @pl.when(k + 3 < NK)
        def _():
            way.forward(k + 3)

        @pl.when(k + 2 < NK)
        def _():
            way.hand_over(k + 2)

    def chunk(k, c):
        gather(k)

        half = parts // 2 - 1

        def pair(i, c):
            for slot in range(2):
                product(k, 2 * i + slot, slot)
                if slot == half % 2:
                    pl.when(i == half // 2)(lambda: middle(k))
            return c

        lax.fori_loop(0, parts // 2, pair, 0)
        end(k)
        return c

    lax.fori_loop(0, NK, chunk, 0)

    def store(n, r, run):
        rows = slice(N * at[r], N * (at[r] + caps[r]))
        run(pltpu.make_async_copy(z.at[rows], h.at[rows, pl.ds(pl.multiple_of(n * KB, KB), KB)], z_sem.at[r]))

    def finish(n, c):
        lanes = pl.ds(pl.multiple_of(n * KB, KB), KB)
        for r in range(E):
            rows = slice(N * at[r], N * (at[r] + caps[r]))

            @pl.when(n > 0)
            def _():
                store(n - 1, r, wait)

            z[rows] = (jax.nn.silu(acc_g[rows, lanes]) * acc_u[rows, lanes]).astype(BF16)
            store(n, r, start)
        return c

    lax.fori_loop(0, FF // KB, finish, 0)
    for r in range(E):
        store(FF // KB - 1, r, wait)

    way.across(2, way.dg, EARLY - 1, wait_send)

    def drain(k, c):
        way.own(k, wait_send)
        way.passed_on(k, wait_send)
        return c

    lax.fori_loop(EARLY, NK, drain, 0)


def down_kernel(
    caps, plan, h, tables, wd, sh, sd, y,
    hv, w0, w1, sv, shv, tv, comb, out, d_out, d_in, p_out, p_in, q_out, q_in, part, own, yv,
    h_sem, w_sem, s_sem, m_sem, y_sem, d_send, d_recv, p_send, p_recv, q_send, q_recv,
):
    seg, at = sum(caps), bases(caps)
    me = lax.axis_index("ep")
    cn, xn, yn, dg = around(me)
    perm = ranks(caps, plan)

    def lanes(n):
        return pl.ds(pl.multiple_of(n * CB, CB), CB)

    def buffer(slot):
        return w0.at[slot] if caps == FULL else (w0, w1)[slot]

    def weights(n, slot, run):
        for e in range(E):
            run(pltpu.make_async_copy(wd.at[e, :, lanes(n)], buffer(slot).at[e], w_sem.at[slot, e]))

    def each_slot(n, f):
        if caps == FULL:
            f(lax.rem(n, 2))
        else:
            for slot in range(2):
                pl.when(lax.rem(n, 2) == slot)(functools.partial(f, slot))

    def shared(n, run):
        slot = lax.rem(n, 2)
        run(pltpu.make_async_copy(sd.at[:, lanes(n)], sv.at[slot], s_sem.at[slot]))

    def activations(r, run):
        rows = slice(N * at[r], N * (at[r] + caps[r]))
        run(pltpu.make_async_copy(h.at[rows], hv.at[rows], h_sem.at[r]))

    for r in range(E):
        activations(r, start)
    weights(0, 0, start)
    load_tables = pltpu.make_async_copy(tables, tv, m_sem.at[0])
    load_tables.start()
    load_sh = pltpu.make_async_copy(sh, shv, m_sem.at[1])
    load_sh.start()
    shared(0, start)
    greet((cn, xn, yn))

    def product(slot, r):
        v = dot(hv[N * at[r]:N * (at[r] + caps[r])], buffer(slot)[perm[r]]).astype(BF16)
        for b in range(N):
            out[slot, b, at[r]:at[r] + caps[r]] = v[b * caps[r]:(b + 1) * caps[r]]

    def combines():
        load_tables.wait()
        wide = comb.shape[-1]

        def one(b, c):
            v = []
            for r in range(E):
                key = (lax.broadcasted_iota(jnp.int32, (caps[r], T), 0) + (me * E + perm[r]) * CAP).astype(F32)
                w = jnp.zeros((caps[r], T), F32)
                for j in range(TOP):
                    w = w + jnp.where(tv[b, j:j + 1, :] == key, tv[b, TOP + j:TOP + j + 1, :], 0.0)
                v.append(w)
            v.append(jnp.zeros((wide - seg, T), F32))
            comb[b] = jnp.concatenate(v).T.astype(BF16)
            return c

        lax.fori_loop(0, N, one, 0)
        load_sh.wait()

    def summed(b, n):
        return dot(comb[b][:, :seg], out[lax.rem(n, 2), b])

    left, right = slice(0, HB), slice(HB, CB)

    def to_partner(n, run):
        slot = lax.rem(n, 2)
        run(remote(d_out.at[slot], d_in.at[slot], d_send.at[slot], d_recv.at[n], cn))

    def first_hop(n, run):
        slot = lax.rem(n, 2)
        for i, d in enumerate((xn, yn)):
            run(remote(p_out.at[slot, i], p_in.at[lax.rem(n, 6), i], p_send.at[slot, i], p_recv.at[n, i], d))

    def second_hop(n, run):
        slot = lax.rem(n, 2)
        for i, d in enumerate((yn, xn)):
            run(remote(q_out.at[slot, i], q_in.at[lax.rem(n, 4), i], q_send.at[slot, i], q_recv.at[n, i], d))

    def result(n, run):
        slot = lax.rem(n, 2)
        run(pltpu.make_async_copy(yv.at[slot], y.at[:, lanes(n)], y_sem.at[slot]))

    def for_partner(n, slot):
        for i, b in enumerate((cn,) + around(cn)[1:]):
            d_out[slot, i] = dot(comb[b][:, :seg], out[slot, b]).astype(BF16)

    def for_first(n):
        slot = lax.rem(n, 2)
        v = [summed(b, n) + d_in[slot, i].astype(F32) for i, b in ((3, dg), (1, xn), (2, yn), (0, me))]
        p_out[slot, 0, 1] = v[0][:, left].astype(BF16)
        p_out[slot, 1, 1] = v[0][:, right].astype(BF16)
        p_out[slot, 0, 0] = v[1][:, left].astype(BF16)
        part[lax.rem(n, 3), 1] = v[1][:, right]
        p_out[slot, 1, 0] = v[2][:, right].astype(BF16)
        part[lax.rem(n, 3), 0] = v[2][:, left]
        own[lax.rem(n, 5)] = v[3]

    def for_second(n):
        for i in range(2):
            q_out[lax.rem(n, 2), i] = (part[lax.rem(n, 3), i] + p_in[lax.rem(n, 6), i, 1].astype(F32)).astype(BF16)

    def for_own(n):
        v = own[lax.rem(n, 5)] + dot(shv[...], sv[lax.rem(n, 2)])
        for i, half in enumerate((left, right)):
            w = v[:, half] + p_in[lax.rem(n, 6), i, 0].astype(F32) + q_in[lax.rem(n, 4), i].astype(F32)
            yv[lax.rem(n, 2), :, half] = w.astype(BF16)

    def ready_first(n):
        @pl.when(n >= 2)
        def _():
            first_hop(n - 2, wait_send)

        to_partner(n, wait_recv)

    def ready_second(n):
        @pl.when(n >= 2)
        def _():
            second_hop(n - 2, wait_send)

        first_hop(n, wait_recv)

    def ready_own(n):
        @pl.when(n >= 2)
        def _():
            result(n - 2, wait)

        shared(n, wait)
        second_hop(n, wait_recv)

    stages = (
        (1, ready_first, for_first, first_hop),
        (3, ready_second, for_second, second_hop),
        (5, ready_own, for_own, result),
    )

    def step(i, c):
        @pl.when(i + 1 < NC)
        def _():
            each_slot(i + 1, lambda slot: weights(i + 1, slot, start))

        @pl.when(jnp.logical_and(i >= 5, i - 4 < NC))
        def _():
            shared(i - 4, start)

        @pl.when(i == 0)
        def _():
            for r in range(E):
                activations(r, wait)

        @pl.when(i < NC)
        def _():
            def half(slot):
                weights(i, slot, wait)
                for r in range(E // 2):
                    product(slot, r)

            each_slot(i, half)

        inner = jnp.logical_and(i >= 5, i <= NC)

        @pl.when(inner)
        def _():
            for lag, ready, _, _ in stages:
                ready(i - lag)
            for lag, _, compute, _ in stages:
                compute(i - lag)
            for lag, _, _, go in stages:
                go(i - lag, start)

        @pl.when(jnp.logical_not(inner))
        def _():
            for lag, ready, compute, go in stages:
                n = i - lag

                @pl.when(jnp.logical_and(n >= 0, n < NC))
                def _():
                    ready(n)
                    compute(n)
                    go(n, start)

        @pl.when(i == 0)
        def _():
            combines()

        @pl.when(i < NC)
        def _():
            @pl.when(i >= 2)
            def _():
                to_partner(i - 2, wait_send)

            def half(slot):
                for r in range(E // 2, E):
                    product(slot, r)
                for_partner(i, slot)

            each_slot(i, half)
            to_partner(i, start)

        return c

    lax.fori_loop(0, NC + 5, step, 0)
    for n in (NC - 2, NC - 1):
        to_partner(n, wait_send)
        first_hop(n, wait_send)
        second_hop(n, wait_send)
        result(n, wait)


ANY = pl.BlockSpec(memory_space=pl.ANY)
SMEM = pl.BlockSpec(memory_space=pltpu.SMEM)
DMA = pltpu.SemaphoreType.DMA


def params(i):
    return pltpu.CompilerParams(collective_id=i, has_side_effects=True, vmem_limit_bytes=VMEM_LIMIT)


def share(expert, slot, gate, x, sg, su):
    return pl.pallas_call(
        share_kernel,
        name="share",
        out_shape=(
            jax.ShapeDtypeStruct((N, T, D), BF16),
            jax.ShapeDtypeStruct((N, ROWS, T), F32),
            jax.ShapeDtypeStruct((TOP, 128), jnp.int32),
            jax.ShapeDtypeStruct((T, FF), BF16),
        ),
        in_specs=[pl.BlockSpec(memory_space=pltpu.VMEM)] * 3 + [ANY] * 3,
        out_specs=(ANY,) * 4,
        scratch_shapes=[
            pltpu.VMEM((ROWS, T), F32),
            pltpu.VMEM((N, ROWS, T), F32),
            pltpu.VMEM((TOP, 128), jnp.int32),
            pltpu.VMEM((NK, T, KB), BF16),
            pltpu.VMEM((SRING, 2, KB, FF), BF16),
            pltpu.VMEM((T, FF), F32),
            pltpu.VMEM((T, FF), F32),
            pltpu.VMEM((T, FF), BF16),
            DMA((NK,)),
            DMA((SRING, 2)),
            DMA((3,)),
            DMA((N - 1,)),
            DMA((N - 1,)),
        ]
        + way_semaphores(EARLY),
        compiler_params=params(0),
    )(expert, slot, gate, x, sg, su)


def up(caps, width, identity, plan, x, xg, tables, wg, wu):
    seg = sum(caps)
    return pl.pallas_call(
        functools.partial(up_kernel, caps),
        name="up",
        out_shape=(jax.ShapeDtypeStruct((N, T, D), BF16), jax.ShapeDtypeStruct((N * seg, FF), BF16)),
        input_output_aliases={2: 0},
        in_specs=[SMEM] + [ANY] * 5,
        out_specs=(ANY,) * 2,
        scratch_shapes=[
            pltpu.VMEM((N * seg, FF), F32),
            pltpu.VMEM((N * seg, FF), F32),
            pltpu.VMEM((N * seg, KB), BF16),
            pltpu.VMEM((2, N, T, KB), BF16),
            pltpu.VMEM((E, 2, KB, width), BF16),
            pltpu.VMEM((E, 2, KB, width), BF16),
            pltpu.VMEM((N, seg, T), BF16),
            pltpu.VMEM((N, ROWS, T), F32),
            DMA((2, E, 2)),
            DMA((2, N)),
            DMA((E,)),
            DMA,
        ]
        + way_semaphores(NK),
        compiler_params=params(identity),
    )(plan, x, xg, tables, wg, wu)[1]


def down(caps, identity, plan, h, tables, wd, sh, sd):
    seg = sum(caps)
    return pl.pallas_call(
        functools.partial(down_kernel, caps),
        name="down",
        out_shape=jax.ShapeDtypeStruct((T, D), BF16),
        in_specs=[SMEM] + [ANY] * 5,
        out_specs=ANY,
        scratch_shapes=[
            pltpu.VMEM((N * seg, FF), BF16),
            pltpu.VMEM((2, E, FF, CB) if caps == FULL else (E, FF, CB), BF16),
            pltpu.VMEM((16, 128) if caps == FULL else (E, FF, CB), BF16),
            pltpu.VMEM((2, FF, CB), BF16),
            pltpu.VMEM((T, FF), BF16),
            pltpu.VMEM((N, ROWS, T), F32),
            pltpu.VMEM((N, T, -(-seg // 128) * 128), BF16),
            pltpu.VMEM((2, N, seg, CB), BF16),
            pltpu.VMEM((2, 4, T, CB), BF16),
            pltpu.VMEM((2, 4, T, CB), BF16),
            pltpu.VMEM((2, 2, 2, T, HB), BF16),
            pltpu.VMEM((6, 2, 2, T, HB), BF16),
            pltpu.VMEM((2, 2, T, HB), BF16),
            pltpu.VMEM((4, 2, T, HB), BF16),
            pltpu.VMEM((3, 2, T, HB), F32),
            pltpu.VMEM((5, T, CB), F32),
            pltpu.VMEM((2, T, CB), BF16),
            DMA((E,)),
            DMA((2, E)),
            DMA((2,)),
            DMA((2,)),
            DMA((2,)),
            DMA((2,)),
            DMA((NC,)),
            DMA((2, 2)),
            DMA((NC, 2)),
            DMA((2, 2)),
            DMA((NC, 2)),
        ],
        compiler_params=params(identity),
    )(plan, h, tables, wd, sh, sd)


def solution(mesh):
    def device(x, expert, slot, gate, wg, wu, wd, sg, su, sd):
        x, expert, slot, gate = x[0, 0], expert[0, 0], slot[0, 0], gate[0, 0]
        xg, tables, plan, sh = share(expert.T, slot.T, gate.T, x, sg, su)

        def experts(caps, width, identity):
            h = up(caps, width, identity, plan, x, xg, tables, wg, wu)
            return down(caps, identity + 1, plan, h, tables, wd, sh, sd)

        y = lax.cond(plan[0, E] == 0, lambda: experts(NARROW, 1024, 1), lambda: experts(FULL, 512, 3))
        return y[None, None]

    tokens, experts = P("dp", "ep"), P("ep")
    return jax.shard_map(
        device,
        mesh=mesh,
        in_specs=(tokens,) * 4 + (experts,) * 3 + (P(),) * 3,
        out_specs=tokens,
        check_vma=False,
    )
```

time: 1170 us -> 345 us (0.29)
  blocking collectives: 408 us -> 0 us
  waiting for transfers between devices: 365 us -> 0 us
  matrix products: 361 us -> 0 us
  Pallas kernels: 0 us -> 339 us
  local copies, waits for them, and re-layouts: 26.9 us -> 5.36 us
    another operation x1 -> x0, blocking collectives: 408 us -> none  [placed(): return lax.with_sharding_constraint(v, NamedSharding(mesh, P(*spec)))]
    another operation x1 -> x0, waiting for transfers between devices: 365 us -> none  [placed(): return lax.with_sharding_constraint(v, NamedSharding(mesh, P(*spec)))]
    dot_general x10 -> x0, matrix products: 361 us -> none  [einsum(): return jnp.einsum(form, a.astype(jnp.float32), b.astype(jnp.float32))]
    pallas_call x0 -> x3, Pallas kernels: none -> 339 us  [the longest x1 168 us: up(): pl.pallas_call(functools.partial(up_kernel, caps), name='up', out_shape=(...]
    another operation x1 -> x0, local copies, waits for them, and re-layouts: 25 us -> none  [placed(): return lax.with_sharding_constraint(v, NamedSharding(mesh, P(*spec)))]
  transfers between devices with their start and end apart: 1 -> 0, of which waited for: 1 -> 0; matrix products, arithmetic and copies ran while one was open for 3% -> 0% of each run, Pallas kernels for 0% -> 0%
where the time goes in v2:
time: 345 us
  Pallas kernels  339 us (98%)
  local copies, waits for them, and re-layouts  5.36 us (2%)
    pallas_call x1, Pallas kernels, up(): pl.pallas_call(functools.partial(up_kernel, caps), name='up', out_shape=(...  168 us
    pallas_call x1, Pallas kernels, down(): pl.pallas_call(functools.partial(down_kernel, caps), name='down', out_sha...  142 us
    pallas_call x1, Pallas kernels, share(): pl.pallas_call(share_kernel, name='share', out_shape=(jax.ShapeDtypeStruc...  28.6 us

profile of v2, /device:TPU:0, one launch (start us, length us, event | category | flops | bytes accessed | tf_op | source)
XLA Modules:
  0.0 345.1 jit_solution(1136658750776711695)
XLA Ops:
  0.0 28.6 %share.1 = (bf16[8,256,7168]{2,1,0:T(8,128)(2,1)}, f32[8,24,256]{2,1,0:T(8,128)}, s32[8,128]{1,0:T(8,128)}, bf16[256,2048]{1,0:T(8,128)(2,1)}) custom-call(s32[8,256]{1,0:T(8,128)} %bitcast.18, s32[8,256]{1,0:T(8,128)} %bitcast.19, f32[8,256]{1,0:T(8,128)} %bitcast.20, bf16[256,7168]{1,0:T(8,128)(2,1)} %bitcast.13, bf16[7168,2048]{1,0:T(8,128)(2,1)} %sg.1, ...), custom_call_target="tpu_custom_call" | custom-call | tf_op jit(solution)/shard_map/share/pallas_call | solution.py:646
  28.6 1.3 slice.3
  30.5 310.5 %conditional.1 = (bf16[1,1,256,7168]{3,2,1,0:T(8,128)(2,1)}) conditional(s32[]{:T(128)} %bitcast.9, (s32[8,128]{1,0:T(8,128)}, bf16[256,7168]{1,0:T(8,128)(2,1)}, bf16[8,256,7168]{2,1,0:T(8,128)(2,1)}, f32[8,24,256]{2,1,0:T(8,128)}, bf16[4,7168,2048]{2,1,0:T(8,128)(2,1)}, /*index=5*/bf16[4,7168,2048]{2,1,0:T(8,128)(2,1)}, ...), branch_computations={%region_0.0_spmd, %region_1.0_spmd} | conditional | bytes 8 | solution.py:756
  30.7 168.0 %up.3 = (bf16[8,256,7168]{2,1,0:T(8,128)(2,1)}, bf16[2176,2048]{1,0:T(8,128)(2,1)}) custom-call(s32[8,128]{1,0:T(8,128)} %get-tuple-element.55.plan, bf16[256,7168]{1,0:T(8,128)(2,1)} %get-tuple-element.56.x, bf16[8,256,7168]{2,1,0:T(8,128)(2,1)} %get-tuple-element.57._, f32[8,24,256]{2,1,0:T(8,128)} %get-tuple-element.58.tables, ...), custom_call_target="tpu_custom_call", output_to_operand_aliasing={{0}: (2, {})} | custom-call | tf_op jit(solution)/shard_map/cond/branch_1_fun/up/pallas_call | solution.py:679
  198.8 142.0 %down.3 = bf16[256,7168]{1,0:T(8,128)(2,1)} custom-call(s32[8,128]{1,0:T(8,128)} %get-tuple-element.55.plan, bf16[2176,2048]{1,0:T(8,128)(2,1)} %get-tuple-element.61.h, f32[8,24,256]{2,1,0:T(8,128)} %get-tuple-element.58.tables, bf16[4,2048,7168]{2,1,0:T(8,128)(2,1)} %get-tuple-element.62.wd, bf16[256,2048]{1,0:T(8,128)(2,1)} %get-tuple-element.63.sh, ...), custom_call_target="tpu_custom_call" | custom-call | tf_op jit(solution)/shard_map/cond/branch_1_fun/down/pallas_call | solution.py:707
  341.0 4.1 %copy.20 = bf16[1,1,256,7168]{3,2,1,0:T(8,128)(2,1)} copy(bf16[1,1,256,7168]{3,2,1,0:T(8,128)(2,1)} %get-tuple-element.73) | data formatting | bytes 7340032

commit v3 on v2

--- a/solution.py
+++ b/solution.py
@@ -76,10 +76,13 @@
         for i, d in enumerate((self.xn, self.yn, self.cn)):
             run(remote(self.x.at[:, cols(k)], self.part(self.me, k), self.o_send.at[i, k], self.o_recv.at[i, k], d))
 
+    def half(self, b, k, i):
+        return self.xg.at[b, :, pl.ds(pl.multiple_of(k * KB + i * (KB // 2), KB // 2), KB // 2)]
+
     def onward(self, k, run):
-        p = lax.rem(k, 2)
-        src, to = self.xn * (1 - p) + self.yn * p, self.yn * (1 - p) + self.xn * p
-        run(remote(self.part(src, k), self.part(src, k), self.f_send.at[k], self.f_recv.at[k], to))
+        for i, (src, to) in enumerate(((self.xn, self.yn), (self.yn, self.xn))):
+            part = self.half(src, k, i)
+            run(remote(part, part, self.f_send.at[i, k], self.f_recv.at[i, k], to))
 
     def across(self, i, src, k, run):
         part = self.part(src, k)
@@ -92,41 +95,45 @@
     def forward(self, k):
         self.arrived(0, self.xn, k)
         self.arrived(1, self.yn, k)
+        self.pass_on(k)
+
+    def pass_on(self, k):
         self.onward(k, start)
         self.across(0, self.xn, k, start)
         self.across(1, self.yn, k, start)
 
     def landed(self, k):
-        part = self.part(self.dg, k)
-        remote(part, part, self.f_send.at[k], self.f_recv.at[k], self.xn).wait_recv()
+        for i, src in enumerate((self.yn, self.xn)):
+            part = self.half(self.dg, k, i)
+            remote(part, part, self.f_send.at[i, k], self.f_recv.at[i, k], src).wait_recv()
 
     def hand_over(self, k):
         self.landed(k)
         self.across(2, self.dg, k, start)
 
-    def across_landed(self, i, k):
-        part = self.part(self.cn, k)
-        remote(part, part, self.c_send.at[i, k], self.c_recv.at[i, k], self.cn).wait_recv()
-
     def complete(self, k):
         self.arrived(2, self.cn, k)
+        self.crossed(k)
+
+    def crossed(self, k):
         for i in range(3):
-            self.across_landed(i, k)
-
-    def passed_on(self, k, run):
-        self.onward(k, run)
+            part = self.part(self.cn, k)
+            remote(part, part, self.c_send.at[i, k], self.c_recv.at[i, k], self.cn).wait_recv()
+
+    def drain(self, k):
+        self.onward(k, wait_send)
         for i, src in enumerate((self.xn, self.yn, self.dg)):
-            self.across(i, src, k, run)
+            self.across(i, src, k, wait_send)
 
 
 def way_semaphores(chunks):
     dma = pltpu.SemaphoreType.DMA
-    return [dma((3, chunks)), dma((3, chunks)), dma((chunks,)), dma((chunks,)), dma((3, chunks)), dma((3, chunks))]
+    return [dma((3, chunks)), dma((3, chunks)), dma((2, chunks)), dma((2, chunks)), dma((3, chunks)), dma((3, chunks))]
 
 
 def share_kernel(
-    expert, slot, gate, x, sg, su, xg, tables, plan, sh,
-    mine, tv, pv, xv, wv, acc_g, acc_u, hv, x_sem, w_sem, h_sem, t_send, t_recv, *sems,
+    expert, slot, gate, x, sg, su, xg, tables, picks, plan, wide, sh,
+    mine, tv, pv, pick, xv, wv, acc_g, acc_u, hv, x_sem, w_sem, h_sem, t_send, t_recv, *sems,
 ):
     me = lax.axis_index("ep")
     others = [lax.rem(me + d, N) for d in range(1, N)]
@@ -157,49 +164,74 @@
     mine[2 * TOP:] = jnp.broadcast_to(jnp.concatenate([used, used], axis=1), (TOP, T))
 
     greet(others)
+    for i, d in enumerate(others):
+        remote(mine, tv.at[me], t_send.at[i], t_recv.at[N - 2 - i], d).start()
     for k in range(EARLY):
         way.own(k, start)
-    for i, d in enumerate(others):
-        remote(mine, tv.at[me], t_send.at[i], t_recv.at[N - 2 - i], d).start()
     for s in range(SRING - 1, NK):
         tokens(s, start)
     tv[me] = mine[...]
 
-    def step(s, first):
-        @pl.when(s + SRING - 1 < NK)
-        def _():
-            weights(s + SRING - 1, start)
-
-        tokens(s, wait)
-        weights(s, wait)
+    def project(s):
         for n in range(FF // NB):
             b = slice(n * NB, (n + 1) * NB)
             for half, acc in ((0, acc_g), (1, acc_u)):
-                v = dot(xv[s], wv[lax.rem(s, SRING), half, :, b])
-                acc[:, b] = v if first else acc[:, b] + v
-
-    step(0, True)
-
-    def body(s, c):
-        step(s, False)
-
-        @pl.when(s == 5)
-        def _():
-            way.forward(0)
-
-        @pl.when(s == 9)
-        def _():
-            way.forward(1)
-
+                acc[:, b] = acc[:, b] + dot(xv[s], wv[lax.rem(s, SRING), half, :, b])
+
+    def ready(s):
+        @pl.when(s + SRING - 1 < NK)
+        def _():
+            weights(s + SRING - 1, start)
+
+        tokens(s, wait)
+        weights(s, wait)
+
+    acc_g[...] = jnp.zeros((T, FF), F32)
+    acc_u[...] = jnp.zeros((T, FF), F32)
+
+    def first_steps(s, c):
+        ready(s)
+        project(s)
         return c
 
-    lax.fori_loop(1, NK, body, 0)
-    for i in range(N - 1):
-        b = lax.rem(me + 1 + i, N)
+    lax.fori_loop(0, NK - N - 1, first_steps, 0)
+    for i, b in enumerate(others):
         remote(mine, tv.at[b], t_send.at[i], t_recv.at[i], b).wait_recv()
     keep = pltpu.make_async_copy(tv, tables, h_sem.at[0])
     keep.start()
-    way.hand_over(0)
+
+    row = (lax.broadcasted_iota(jnp.int32, (SEG, T), 0) + me * SEG).astype(F32)
+
+    def last_steps(s, c):
+        ready(s)
+        b = jnp.minimum(s - (NK - N - 1), N - 1)
+        hit = tv[b, :1, :] == row
+        for j in range(1, TOP):
+            hit = hit | (tv[b, j:j + 1, :] == row)
+        hit = jnp.where(hit, 1.0, 0.0).astype(BF16)
+        for e in range(E):
+            pick[b, e] = hit[e * CAP:(e + 1) * CAP]
+        project(s)
+
+        @pl.when(s == 6)
+        def _():
+            way.forward(0)
+
+        @pl.when(s == 9)
+        def _():
+            way.forward(1)
+            way.own(2, start)
+
+        @pl.when(s == 12)
+        def _():
+            way.hand_over(0)
+
+        return c
+
+    lax.fori_loop(NK - N - 1, NK, last_steps, 0)
+    keep_picks = pltpu.make_async_copy(pick, picks, h_sem.at[3])
+    keep_picks.start()
+    way.hand_over(1)
 
     n = tv[0, 2 * TOP:, :128]
     for b in range(1, N):
@@ -214,8 +246,8 @@
     caps = jnp.zeros(n.shape, F32)
     for r in range(E):
         caps = jnp.where(rank == r, float(NARROW[r]), caps)
-    over = jnp.where((n > caps) & (lane < EXPERTS), 1.0, 0.0)
-    out = jnp.where(lane == E, jnp.max(over, axis=1, keepdims=True), 0.0)
+    wide[0] = jnp.max(jnp.where((n > caps) & (lane < EXPERTS), 1.0, 0.0)).astype(jnp.int32)
+    out = jnp.zeros(n.shape, F32)
     for r in range(E):
         chosen = jnp.where((lane // E == me) & (rank == r), e, 0).astype(F32)
         out = out + jnp.where(lane == r, jnp.sum(chosen, axis=1, keepdims=True), 0.0)
@@ -228,20 +260,31 @@
     keep_sh.start()
     for i, d in enumerate(others):
         remote(mine, tv.at[me], t_send.at[i], t_recv.at[N - 2 - i], d).wait_send()
-    way.complete(0)
-    way.across(2, way.dg, 0, wait_send)
-    way.arrived(2, way.cn, 1)
-    way.landed(1)
     for k in range(EARLY):
+        way.complete(k)
         way.own(k, wait_send)
-        way.onward(k, wait_send)
-        for i, src in enumerate((way.xn, way.yn)):
-            way.across(i, src, k, wait_send)
-    for i in range(2):
-        way.across_landed(i, 1)
+        way.drain(k)
+    for i, src in enumerate((way.xn, way.yn, way.cn)):
+        way.arrived(i, src, EARLY)
+    way.own(EARLY, wait_send)
     keep.wait()
     keep_plan.wait()
+    keep_picks.wait()
     keep_sh.wait()
+
+
+def buffers(caps, w0, w1):
+    full = caps == FULL
+    buffer = lambda slot: w0.at[slot] if full else (w0, w1)[slot]
+
+    def in_slot(slot, f):
+        if full or isinstance(slot, int):
+            f(slot)
+        else:
+            for q in range(2):
+                pl.when(slot == q)(functools.partial(f, q))
+
+    return buffer, in_slot
 
 
 def bases(caps):
@@ -253,23 +296,24 @@
 
 
 def up_kernel(
-    caps, plan, x, _, tables, wg, wu, xg, h, acc_g, acc_u, z, xv, w0, w1, pick, tv, w_sem, x_sem, z_sem, t_sem, *sems
+    caps, plan, x, _, picks, wg, wu, xg, h, acc_g, acc_u, z, xv, w0, w1, pick, w_sem, x_sem, z_sem, p_sem, *sems
 ):
     seg, at = sum(caps), bases(caps)
-    wv = (w0, w1)
     width = w0.shape[-1]
     parts = FF // width
     me = lax.axis_index("ep")
     way = Way(x, xg, sems)
     perm = ranks(caps, plan)
-
-    def weights(s, slot, run):
-        @pl.when(s < NK * parts)
-        def _():
+    buffer, in_slot = buffers(caps, w0, w1)
+
+    def weights(s, run):
+        def copies(slot):
             k, lanes = s // parts, pl.ds(pl.multiple_of(lax.rem(s, parts) * width, width), width)
             for e in range(E):
                 for half, ref in ((0, wg), (1, wu)):
-                    run(pltpu.make_async_copy(ref.at[e, cols(k), lanes], wv[slot].at[e, half], w_sem.at[slot, e, half]))
+                    run(pltpu.make_async_copy(ref.at[e, cols(k), lanes], buffer(slot).at[e, half], w_sem.at[slot, e, half]))
+
+        pl.when(s < NK * parts)(lambda: in_slot(lax.rem(s, 2), copies))
 
     def tokens(k, run):
         slot = lax.rem(k, 2)
@@ -281,81 +325,64 @@
                 run(pltpu.make_async_copy(way.part(b, k), xv.at[slot, b], x_sem.at[slot, b]))
             run(pltpu.make_async_copy(x.at[:, cols(k)], xv.at[slot, me], x_sem.at[slot, me]))
 
-    load_tables = pltpu.make_async_copy(tables, tv, t_sem)
-    load_tables.start()
+    load_picks = pltpu.make_async_copy(picks, pick, p_sem)
+    load_picks.start()
     tokens(0, start)
-    weights(0, 0, start)
+    weights(0, start)
+    tokens(1, start)
     greet((way.cn, way.xn, way.yn))
-    way.across(2, way.dg, EARLY - 1, start)
-    for k in range(EARLY, EARLY + 2):
-        way.own(k, start)
-
-    load_tables.wait()
-    first_key = [(me * E + perm[r]) * CAP for r in range(E)]
-
-    def picks(b, c):
-        for r in range(E):
-            key = (lax.broadcasted_iota(jnp.int32, (caps[r], T), 0) + first_key[r]).astype(F32)
-            hit = jnp.zeros((caps[r], T), F32)
-            for j in range(TOP):
-                hit = hit + jnp.where(tv[b, j:j + 1, :] == key, 1.0, 0.0)
-            pick[b, at[r]:at[r] + caps[r]] = hit.astype(BF16)
+    way.pass_on(EARLY)
+    way.own(EARLY + 1, start)
+    way.own(EARLY + 2, start)
+
+    def clear(i, c):
+        rows = pl.ds(pl.multiple_of(i * 64, 64), 64)
+        acc_g[rows] = jnp.zeros((64, FF), F32)
+        acc_u[rows] = jnp.zeros((64, FF), F32)
         return c
 
-    lax.fori_loop(0, N, picks, 0)
-
-    def clear(i, c):
-        rows = pl.ds(pl.multiple_of(i * 16, 16), 16)
-        acc_g[rows] = jnp.zeros((16, FF), F32)
-        acc_u[rows] = jnp.zeros((16, FF), F32)
-        return c
-
-    lax.fori_loop(0, N * seg // 16, clear, 0)
+    lax.fori_loop(0, N * seg // 64, clear, 0)
+    load_picks.wait()
 
     def gather(k):
         slot = lax.rem(k, 2)
         tokens(k, wait)
         for b in range(N):
-            v = dot(pick[b], xv[slot, b]).astype(BF16)
+            hit = jnp.concatenate([pick[b, perm[r]][:caps[r]] for r in range(E)])
+            v = dot(hit, xv[slot, b]).astype(BF16)
             for r in range(E):
                 z[N * at[r] + b * caps[r]:N * at[r] + (b + 1) * caps[r]] = v[at[r]:at[r] + caps[r]]
 
-    def product(k, j, slot):
+    def product(k, j):
         s = k * parts + j
-        weights(s + 1, 1 - slot, start)
-        weights(s, slot, wait)
-        for n in range(width // NB):
-            b = pl.ds(pl.multiple_of(j * width + n * NB, NB), NB)
-            for r in range(E):
-                rows = slice(N * at[r], N * (at[r] + caps[r]))
-                for half, acc in ((0, acc_g), (1, acc_u)):
-                    acc[rows, b] = acc[rows, b] + dot(
-                        z[rows], wv[slot][perm[r], half, :, n * NB:(n + 1) * NB]
-                    )
-
-    def bring(k):
-        @pl.when(k < NK)
-        def _():
-            @pl.when(k >= EARLY)
-            def _():
-                way.complete(k)
-
-            @pl.when(k == EARLY - 1)
-            def _():
-                way.across_landed(2, k)
-
-            tokens(k, start)
+        weights(s + 1, start)
+        weights(s, wait)
+
+        def add(slot):
+            for n in range(width // NB):
+                b = pl.ds(pl.multiple_of(j * width + n * NB, NB), NB)
+                for r in range(E):
+                    rows = slice(N * at[r], N * (at[r] + caps[r]))
+                    for half, acc in ((0, acc_g), (1, acc_u)):
+                        w = buffer(slot)[perm[r], half, :, n * NB:(n + 1) * NB]
+                        acc[rows, b] = acc[rows, b] + dot(z[rows], w)
+
+        in_slot(lax.rem(s, 2), add)
 
     def middle(k):
-        @pl.when(k == 0)
-        def _():
-            way.forward(EARLY)
-
-        @pl.when(k + 4 < NK)
-        def _():
-            way.own(k + 4, start)
-
-        bring(k + 1)
+        @pl.when(k + 5 < NK)
+        def _():
+            way.own(k + 5, start)
+
+        @pl.when(k + 1 == EARLY)
+        def _():
+            way.crossed(EARLY)
+
+        @pl.when(jnp.logical_and(k + 1 > EARLY, k + 1 < NK))
+        def _():
+            way.complete(k + 1)
+
+        pl.when(k + 1 >= EARLY)(lambda: tokens(k + 1, start))
 
     def end(k):
         @pl.when(k + 3 < NK)
@@ -369,16 +396,12 @@
     def chunk(k, c):
         gather(k)
 
-        half = parts // 2 - 1
-
-        def pair(i, c):
-            for slot in range(2):
-                product(k, 2 * i + slot, slot)
-                if slot == half % 2:
-                    pl.when(i == half // 2)(lambda: middle(k))
+        def part(j, c):
+            product(k, j)
+            pl.when(j == parts // 2 - 1)(lambda: middle(k))
             return c
 
-        lax.fori_loop(0, parts // 2, pair, 0)
+        lax.fori_loop(0, parts, part, 0)
         end(k)
         return c
 
@@ -405,11 +428,9 @@
     for r in range(E):
         store(FF // KB - 1, r, wait)
 
-    way.across(2, way.dg, EARLY - 1, wait_send)
-
     def drain(k, c):
-        way.own(k, wait_send)
-        way.passed_on(k, wait_send)
+        pl.when(k > EARLY)(lambda: way.own(k, wait_send))
+        way.drain(k)
         return c
 
     lax.fori_loop(EARLY, NK, drain, 0)
@@ -428,19 +449,14 @@
     def lanes(n):
         return pl.ds(pl.multiple_of(n * CB, CB), CB)
 
-    def buffer(slot):
-        return w0.at[slot] if caps == FULL else (w0, w1)[slot]
-
-    def weights(n, slot, run):
-        for e in range(E):
-            run(pltpu.make_async_copy(wd.at[e, :, lanes(n)], buffer(slot).at[e], w_sem.at[slot, e]))
-
-    def each_slot(n, f):
-        if caps == FULL:
-            f(lax.rem(n, 2))
-        else:
-            for slot in range(2):
-                pl.when(lax.rem(n, 2) == slot)(functools.partial(f, slot))
+    buffer, in_slot = buffers(caps, w0, w1)
+
+    def weights(n, run):
+        def copies(slot):
+            for e in range(E):
+                run(pltpu.make_async_copy(wd.at[e, :, lanes(n)], buffer(slot).at[e], w_sem.at[slot, e]))
+
+        in_slot(n % 2, copies)
 
     def shared(n, run):
         slot = lax.rem(n, 2)
@@ -450,11 +466,11 @@
         rows = slice(N * at[r], N * (at[r] + caps[r]))
         run(pltpu.make_async_copy(h.at[rows], hv.at[rows], h_sem.at[r]))
 
+    load_tables = pltpu.make_async_copy(tables, tv, m_sem.at[0])
+    load_tables.start()
+    weights(0, start)
     for r in range(E):
         activations(r, start)
-    weights(0, 0, start)
-    load_tables = pltpu.make_async_copy(tables, tv, m_sem.at[0])
-    load_tables.start()
     load_sh = pltpu.make_async_copy(sh, shv, m_sem.at[1])
     load_sh.start()
     shared(0, start)
@@ -475,14 +491,15 @@
                 key = (lax.broadcasted_iota(jnp.int32, (caps[r], T), 0) + (me * E + perm[r]) * CAP).astype(F32)
                 w = jnp.zeros((caps[r], T), F32)
                 for j in range(TOP):
-                    w = w + jnp.where(tv[b, j:j + 1, :] == key, tv[b, TOP + j:TOP + j + 1, :], 0.0)
+                    w = jnp.where(tv[b, j:j + 1, :] == key, tv[b, TOP + j:TOP + j + 1, :], w)
                 v.append(w)
             v.append(jnp.zeros((wide - seg, T), F32))
             comb[b] = jnp.concatenate(v).T.astype(BF16)
             return c
 
         lax.fori_loop(0, N, one, 0)
-        load_sh.wait()
+
+    combines()
 
     def summed(b, n):
         return dot(comb[b][:, :seg], out[lax.rem(n, 2), b])
@@ -563,7 +580,7 @@
     def step(i, c):
         @pl.when(i + 1 < NC)
         def _():
-            each_slot(i + 1, lambda slot: weights(i + 1, slot, start))
+            weights(i + 1, start)
 
         @pl.when(jnp.logical_and(i >= 5, i - 4 < NC))
         def _():
@@ -571,17 +588,19 @@
 
         @pl.when(i == 0)
         def _():
+            load_sh.wait()
             for r in range(E):
                 activations(r, wait)
 
         @pl.when(i < NC)
         def _():
+            weights(i, wait)
+
             def half(slot):
-                weights(i, slot, wait)
                 for r in range(E // 2):
                     product(slot, r)
 
-            each_slot(i, half)
+            in_slot(lax.rem(i, 2), half)
 
         inner = jnp.logical_and(i >= 5, i <= NC)
 
@@ -605,10 +624,6 @@
                     compute(n)
                     go(n, start)
 
-        @pl.when(i == 0)
-        def _():
-            combines()
-
         @pl.when(i < NC)
         def _():
             @pl.when(i >= 2)
@@ -620,7 +635,7 @@
                     product(slot, r)
                 for_partner(i, slot)
 
-            each_slot(i, half)
+            in_slot(lax.rem(i, 2), half)
             to_partner(i, start)
 
         return c
@@ -649,15 +664,18 @@
         out_shape=(
             jax.ShapeDtypeStruct((N, T, D), BF16),
             jax.ShapeDtypeStruct((N, ROWS, T), F32),
+            jax.ShapeDtypeStruct((N, E, CAP, T), BF16),
             jax.ShapeDtypeStruct((TOP, 128), jnp.int32),
+            jax.ShapeDtypeStruct((1,), jnp.int32),
             jax.ShapeDtypeStruct((T, FF), BF16),
         ),
         in_specs=[pl.BlockSpec(memory_space=pltpu.VMEM)] * 3 + [ANY] * 3,
-        out_specs=(ANY,) * 4,
+        out_specs=(ANY,) * 4 + (SMEM, ANY),
         scratch_shapes=[
             pltpu.VMEM((ROWS, T), F32),
             pltpu.VMEM((N, ROWS, T), F32),
             pltpu.VMEM((TOP, 128), jnp.int32),
+            pltpu.VMEM((N, E, CAP, T), BF16),
             pltpu.VMEM((NK, T, KB), BF16),
             pltpu.VMEM((SRING, 2, KB, FF), BF16),
             pltpu.VMEM((T, FF), F32),
@@ -665,16 +683,16 @@
             pltpu.VMEM((T, FF), BF16),
             DMA((NK,)),
             DMA((SRING, 2)),
-            DMA((3,)),
+            DMA((4,)),
             DMA((N - 1,)),
             DMA((N - 1,)),
         ]
-        + way_semaphores(EARLY),
+        + way_semaphores(EARLY + 1),
         compiler_params=params(0),
     )(expert, slot, gate, x, sg, su)
 
 
-def up(caps, width, identity, plan, x, xg, tables, wg, wu):
+def up(caps, width, identity, plan, x, xg, picks, wg, wu):
     seg = sum(caps)
     return pl.pallas_call(
         functools.partial(up_kernel, caps),
@@ -688,10 +706,9 @@
             pltpu.VMEM((N * seg, FF), F32),
             pltpu.VMEM((N * seg, KB), BF16),
             pltpu.VMEM((2, N, T, KB), BF16),
-            pltpu.VMEM((E, 2, KB, width), BF16),
-            pltpu.VMEM((E, 2, KB, width), BF16),
-            pltpu.VMEM((N, seg, T), BF16),
-            pltpu.VMEM((N, ROWS, T), F32),
+            pltpu.VMEM((2, E, 2, KB, width) if caps == FULL else (E, 2, KB, width), BF16),
+            pltpu.VMEM((16, 128) if caps == FULL else (E, 2, KB, width), BF16),
+            pltpu.VMEM((N, E, CAP, T), BF16),
             DMA((2, E, 2)),
             DMA((2, N)),
             DMA((E,)),
@@ -699,7 +716,7 @@
         ]
         + way_semaphores(NK),
         compiler_params=params(identity),
-    )(plan, x, xg, tables, wg, wu)[1]
+    )(plan, x, xg, picks, wg, wu)[1]
 
 
 def down(caps, identity, plan, h, tables, wd, sh, sd):
@@ -747,13 +764,13 @@
 def solution(mesh):
     def device(x, expert, slot, gate, wg, wu, wd, sg, su, sd):
         x, expert, slot, gate = x[0, 0], expert[0, 0], slot[0, 0], gate[0, 0]
-        xg, tables, plan, sh = share(expert.T, slot.T, gate.T, x, sg, su)
+        xg, tables, picks, plan, wide, sh = share(expert.T, slot.T, gate.T, x, sg, su)
 
         def experts(caps, width, identity):
-            h = up(caps, width, identity, plan, x, xg, tables, wg, wu)
+            h = up(caps, width, identity, plan, x, xg, picks, wg, wu)
             return down(caps, identity + 1, plan, h, tables, wd, sh, sd)
 
-        y = lax.cond(plan[0, E] == 0, lambda: experts(NARROW, 1024, 1), lambda: experts(FULL, 512, 3))
+        y = lax.switch(wide[0], (lambda: experts(NARROW, 1024, 1), lambda: experts(FULL, 512, 3)))
         return y[None, None]
 
     tokens, experts = P("dp", "ep"), P("ep")

time: 345 us -> 341 us (0.988)
    pallas_call x1, Pallas kernels: 168 us -> 162 us  [up(): pl.pallas_call(functools.partial(up_kernel, caps), name='up', out_shape=(...]
    pallas_call x1, Pallas kernels: 28.6 us -> 33 us  [share(): pl.pallas_call(share_kernel, name='share', out_shape=(jax.ShapeDtypeStruc...]
where the time goes in v3:
time: 341 us
  Pallas kernels  336 us (99%)
  local copies, waits for them, and re-layouts  4.11 us (1%)
    pallas_call x1, Pallas kernels, up(): pl.pallas_call(functools.partial(up_kernel, caps), name='up', out_shape=(...  162 us
    pallas_call x1, Pallas kernels, down(): pl.pallas_call(functools.partial(down_kernel, caps), name='down', out_sha...  140 us
    pallas_call x1, Pallas kernels, share(): pl.pallas_call(share_kernel, name='share', out_shape=(jax.ShapeDtypeStruc...  33 us

profile of v3, /device:TPU:0, one launch (start us, length us, event | category | flops | bytes accessed | tf_op | source)
XLA Modules:
  0.0 340.9 jit_solution(16694227391286365129)
XLA Ops:
  0.0 33.0 %share.1 = (bf16[8,256,7168]{2,1,0:T(8,128)(2,1)}, f32[8,24,256]{2,1,0:T(8,128)}, bf16[8,4,80,256]{3,2,1,0:T(8,128)(2,1)}, s32[8,128]{1,0:T(8,128)}, s32[1]{0:T(128)}, /*index=5*/bf16[256,2048]{1,0:T(8,128)(2,1)}) custom-call(s32[8,256]{1,0:T(8,128)} %bitcast.18, s32[8,256]{1,0:T(8,128)} %bitcast.19, f32[8,256]{1,0:T(8,128)} %bitcast.20, ...), custom_call_target="tpu_custom_call" | custom-call | tf_op jit(solution)/shard_map/share/pallas_call | solution.py:661
  33.7 303.1 %conditional.1 = (bf16[1,1,256,7168]{3,2,1,0:T(8,128)(2,1)}) conditional(s32[]{:T(128)} %bitcast.9, (s32[8,128]{1,0:T(8,128)}, bf16[256,7168]{1,0:T(8,128)(2,1)}, bf16[8,256,7168]{2,1,0:T(8,128)(2,1)}, bf16[8,4,80,256]{3,2,1,0:T(8,128)(2,1)}, bf16[4,7168,2048]{2,1,0:T(8,128)(2,1)}, /*index=5*/bf16[4,7168,2048]{2,1,0:T(8,128)(2,1)}, ...), branch_computations={%region_0.0_spmd, %region_1.0_spmd} | conditional | bytes 8 | solution.py:773
  33.9 162.3 %up.2 = (bf16[8,256,7168]{2,1,0:T(8,128)(2,1)}, bf16[2176,2048]{1,0:T(8,128)(2,1)}) custom-call(s32[8,128]{1,0:T(8,128)} %get-tuple-element.49.plan, bf16[256,7168]{1,0:T(8,128)(2,1)} %get-tuple-element.50.x, bf16[8,256,7168]{2,1,0:T(8,128)(2,1)} %get-tuple-element.51._, ...), custom_call_target="tpu_custom_call", output_to_operand_aliasing={{0}: (2, {})} | custom-call | tf_op jit(solution)/shard_map/cond/branch_0_fun/up/pallas_call | solution.py:697
  196.2 140.4 %down.2 = bf16[256,7168]{1,0:T(8,128)(2,1)} custom-call(s32[8,128]{1,0:T(8,128)} %get-tuple-element.49.plan, bf16[2176,2048]{1,0:T(8,128)(2,1)} %get-tuple-element.55.h, f32[8,24,256]{2,1,0:T(8,128)} %get-tuple-element.56.tables, bf16[4,2048,7168]{2,1,0:T(8,128)(2,1)} %get-tuple-element.57.wd, bf16[256,2048]{1,0:T(8,128)(2,1)} %get-tuple-element.58.sh, ...), custom_call_target="tpu_custom_call" | custom-call | tf_op jit(solution)/shard_map/cond/branch_0_fun/down/pallas_call | solution.py:724
  336.8 4.1 %copy.20 = bf16[1,1,256,7168]{3,2,1,0:T(8,128)(2,1)} copy(bf16[1,1,256,7168]{3,2,1,0:T(8,128)(2,1)} %get-tuple-element.83) | data formatting | bytes 7340032

commit v4 on v3

--- a/solution.py
+++ b/solution.py
@@ -329,7 +329,6 @@
     load_picks.start()
     tokens(0, start)
     weights(0, start)
-    tokens(1, start)
     greet((way.cn, way.xn, way.yn))
     way.pass_on(EARLY)
     way.own(EARLY + 1, start)
@@ -343,6 +342,7 @@
 
     lax.fori_loop(0, N * seg // 64, clear, 0)
     load_picks.wait()
+    tokens(1, start)
 
     def gather(k):
         slot = lax.rem(k, 2)
@@ -472,8 +472,6 @@
     for r in range(E):
         activations(r, start)
     load_sh = pltpu.make_async_copy(sh, shv, m_sem.at[1])
-    load_sh.start()
-    shared(0, start)
     greet((cn, xn, yn))
 
     def product(slot, r):
@@ -588,9 +586,17 @@
 
         @pl.when(i == 0)
         def _():
-            load_sh.wait()
             for r in range(E):
                 activations(r, wait)
+
+        @pl.when(i == 2)
+        def _():
+            load_sh.start()
+            shared(0, start)
+
+        @pl.when(i == 4)
+        def _():
+            load_sh.wait()
 
         @pl.when(i < NC)
         def _():

time: 341 us -> 342 us (level)
  no operation moved by 1% of the time
where the time goes in v4:
time: 342 us
  Pallas kernels  337 us (99%)
  local copies, waits for them, and re-layouts  4.11 us (1%)
    pallas_call x1, Pallas kernels, up(): pl.pallas_call(functools.partial(up_kernel, caps), name='up', out_shape=(...  162 us
    pallas_call x1, Pallas kernels, down(): pl.pallas_call(functools.partial(down_kernel, caps), name='down', out_sha...  142 us
    pallas_call x1, Pallas kernels, share(): pl.pallas_call(share_kernel, name='share', out_shape=(jax.ShapeDtypeStruc...  33 us

profile of v4, /device:TPU:0, one launch (start us, length us, event | category | flops | bytes accessed | tf_op | source)
XLA Modules:
  0.0 341.8 jit_solution(13304435142301671871)
XLA Ops:
  0.0 33.0 %share.1 = (bf16[8,256,7168]{2,1,0:T(8,128)(2,1)}, f32[8,24,256]{2,1,0:T(8,128)}, bf16[8,4,80,256]{3,2,1,0:T(8,128)(2,1)}, s32[8,128]{1,0:T(8,128)}, s32[1]{0:T(128)}, /*index=5*/bf16[256,2048]{1,0:T(8,128)(2,1)}) custom-call(s32[8,256]{1,0:T(8,128)} %bitcast.18, s32[8,256]{1,0:T(8,128)} %bitcast.19, f32[8,256]{1,0:T(8,128)} %bitcast.20, ...), custom_call_target="tpu_custom_call" | custom-call | tf_op jit(solution)/shard_map/share/pallas_call | solution.py:667
  33.7 304.0 %conditional.1 = (bf16[1,1,256,7168]{3,2,1,0:T(8,128)(2,1)}) conditional(s32[]{:T(128)} %bitcast.9, (s32[8,128]{1,0:T(8,128)}, bf16[256,7168]{1,0:T(8,128)(2,1)}, bf16[8,256,7168]{2,1,0:T(8,128)(2,1)}, bf16[8,4,80,256]{3,2,1,0:T(8,128)(2,1)}, bf16[4,7168,2048]{2,1,0:T(8,128)(2,1)}, /*index=5*/bf16[4,7168,2048]{2,1,0:T(8,128)(2,1)}, ...), branch_computations={%region_0.0_spmd, %region_1.0_spmd} | conditional | bytes 8 | solution.py:779
  33.9 162.0 %up.2 = (bf16[8,256,7168]{2,1,0:T(8,128)(2,1)}, bf16[2176,2048]{1,0:T(8,128)(2,1)}) custom-call(s32[8,128]{1,0:T(8,128)} %get-tuple-element.49.plan, bf16[256,7168]{1,0:T(8,128)(2,1)} %get-tuple-element.50.x, bf16[8,256,7168]{2,1,0:T(8,128)(2,1)} %get-tuple-element.51._, ...), custom_call_target="tpu_custom_call", output_to_operand_aliasing={{0}: (2, {})} | custom-call | tf_op jit(solution)/shard_map/cond/branch_0_fun/up/pallas_call | solution.py:703
  195.9 141.5 %down.2 = bf16[256,7168]{1,0:T(8,128)(2,1)} custom-call(s32[8,128]{1,0:T(8,128)} %get-tuple-element.49.plan, bf16[2176,2048]{1,0:T(8,128)(2,1)} %get-tuple-element.55.h, f32[8,24,256]{2,1,0:T(8,128)} %get-tuple-element.56.tables, bf16[4,2048,7168]{2,1,0:T(8,128)(2,1)} %get-tuple-element.57.wd, bf16[256,2048]{1,0:T(8,128)(2,1)} %get-tuple-element.58.sh, ...), custom_call_target="tpu_custom_call" | custom-call | tf_op jit(solution)/shard_map/cond/branch_0_fun/down/pallas_call | solution.py:730
  337.7 4.1 %copy.20 = bf16[1,1,256,7168]{3,2,1,0:T(8,128)(2,1)} copy(bf16[1,1,256,7168]{3,2,1,0:T(8,128)(2,1)} %get-tuple-element.83) | data formatting | bytes 7340032
